TPU v7x, 32 devices: a whole 2x2x4 slice. The times are simulated.
32 devices in a mesh: row: 4 (over z), col: 8 (over y, x, core).
Axes of the slice: x: 2, y: 2, z: 4, core: 2. Of those that a mesh axis runs over, the one named last changes fastest.
Arguments:
- eigvecs: bfloat16 [40960, 2048], P('row', 'col'), may hold values from -0.125 to 0.125
- reflectors: bfloat16 [2, 40960, 128], P(None, 'row'), may hold values from -6 to 6
- factors: float32 [2, 128, 128], replicated, may hold values from -0.00024414062 to 0.00024414062
- frequencies: float32 [2048], replicated, may hold values from 0.3 to 3
- region_blocks: int32 [72], P('row'), may hold values from 0 to 319, as said below
Outputs:
- covariance: float32 [9216, 9216], P('row', 'col')
Inputs may be any that keep to these rules, and one draw needn't show every extreme that they name: `region_blocks`: the 72 block numbers are distinct and ascending; exactly 18 of them lie in each consecutive run of 80 block numbers.
All inputs are finite; a program needn't handle non-finite values.
Results may differ from a plain program's by a relative error of at most 0.004.
Values may be sent and summed in bfloat16 or wider, within the bound.
A program may use at most 128 MiB of HBM per device.

v0:
```python
import functools

import jax
import jax.numpy as jnp
from jax import lax
from jax.experimental import pallas as pl
from jax.experimental.pallas import tpu as pltpu
from jax.sharding import PartitionSpec as P

BLOCK = 128
MESH = pl.DeviceIdType.MESH
SUB = 12


def contract_rows(left, right):
    return lax.dot_general(
        left, right, (((0,), (0,)), ((), ())), preferred_element_type=jnp.float32
    )


def contract_cols(left, right):
    return lax.dot_general(
        left, right, (((1,), (1,)), ((), ())), preferred_element_type=jnp.float32
    )


def exchange_kernel(
    n_row, sub, x_ref, a_ref, b_ref, half_buf,
    own_sem, send_plane, send_sib, recv_a, send_z, recv_b, fill_sem,
):
    r = lax.axis_index("row")
    c = lax.axis_index("col")
    k = c // 2
    h = lax.rem(c, 2)
    o = 1 - h
    sib = 2 * k + o
    rows, cols = x_ref.shape
    step = rows // sub
    hsub = sub // 2
    half = rows // 2
    has_up = (r < n_row - 1).astype(jnp.int32)
    has_dn = (r > 0).astype(jnp.int32)

    barrier = pltpu.get_barrier_semaphore()

    def greet(row, col):
        pl.semaphore_signal(barrier, inc=1, device_id=(row, col), device_id_type=MESH)

    greet(r, sib)
    for d in range(1, n_row):
        greet(r, 2 * (k ^ d) + h)

    @pl.when(r < n_row - 1)
    def _():
        greet(r + 1, c)

    @pl.when(r > 0)
    def _():
        greet(r - 1, c)

    pl.semaphore_wait(barrier, n_row + has_up + has_dn)

    def piece_cols(d, side):
        owner = 2 * (k ^ d) + (h if side == 0 else o)
        return pl.ds(pl.multiple_of(owner * cols, cols), cols)

    def a_at(d, side, s):
        return a_ref.at[pl.ds(s * step, step), piece_cols(d, side)]

    def plane_copy(d, s):
        return pltpu.make_async_remote_copy(
            src_ref=x_ref.at[pl.ds(s * step, step), :],
            dst_ref=a_ref.at[pl.ds(s * step, step), piece_cols(0, 0)],
            send_sem=send_plane.at[d, s], recv_sem=recv_a.at[d, 0, s],
            device_id=(r, 2 * (k ^ d) + h), device_id_type=MESH,
        )

    def sib_copy(d, s):
        src = x_ref.at[pl.ds(s * step, step), :] if d == 0 else a_at(d, 0, s)
        return pltpu.make_async_remote_copy(
            src_ref=src, dst_ref=a_at(d, 0, s),
            send_sem=send_sib.at[d, s], recv_sem=recv_a.at[d, 1, s],
            device_id=(r, sib), device_id_type=MESH,
        )

    def half_rows(t):
        return pl.ds(pl.multiple_of(h * half + t * step, step), step)

    def z_copy(src, way, target, d, side, t):
        return pltpu.make_async_remote_copy(
            src_ref=src,
            dst_ref=b_ref.at[pl.ds(t * step, step), piece_cols(d, side)],
            send_sem=send_z.at[way, d, side, t], recv_sem=recv_b.at[d, side, t],
            device_id=(target, c), device_id_type=MESH,
        )

    def from_source(way, target, d, side, t):
        if d == 0 and side == 0:
            src = x_ref.at[half_rows(t), :]
        else:
            src = a_ref.at[half_rows(t), piece_cols(d, side)]
        return z_copy(src, way, target, d, side, t)

    def relay(way, target, d, side, t):
        src = b_ref.at[pl.ds(t * step, step), piece_cols(d, side)]
        return z_copy(src, way, target, d, side, t)

    own = pltpu.make_async_copy(x_ref, a_ref.at[:, piece_cols(0, 0)], own_sem)
    own.start()
    for s in range(sub):
        sib_copy(0, s).start()
    for d in range(1, n_row):
        for s in range(sub):
            plane_copy(d, s).start()

    arrivals = [(d, s) for d in range(1, n_row) for s in range(sub)]
    parts = [(d, side, t) for d in range(n_row) for side in (0, 1) for t in range(hsub)]

    def take_a(d, s):
        plane_copy(d, s).wait_recv()
        sib_copy(d, s).start()

    at_source = r == k
    above = r > k
    below = r < k

    @pl.when(at_source)
    def _():
        def push(d, side, t):
            @pl.when(r < n_row - 1)
            def _():
                from_source(0, r + 1, d, side, t).start()

            @pl.when(r > 0)
            def _():
                from_source(1, r - 1, d, side, t).start()

        for d in range(n_row):
            if d:
                for s in range(sub):
                    take_a(d, s)
            else:
                for t in range(hsub):
                    push(d, 0, t)
            for s in range(sub):
                sib_copy(d, s).wait_recv()
            for side in (0, 1) if d else (1,):
                for t in range(hsub):
                    push(d, side, t)
        own.wait()
        fill = pltpu.make_async_copy(
            a_ref.at[pl.ds(pl.multiple_of(h * half, half), half), :], half_buf, fill_sem
        )
        fill.start()
        fill.wait()
        out = pltpu.make_async_copy(half_buf, b_ref, fill_sem)
        out.start()
        out.wait()

    @pl.when(jnp.logical_not(at_source))
    def _():
        for i, (d, side, t) in enumerate(parts):
            if i < len(arrivals):
                take_a(*arrivals[i])
            relay(0, r, d, side, t).wait_recv()

            @pl.when(above & (r < n_row - 1))
            def _():
                relay(0, r + 1, d, side, t).start()

            @pl.when(below & (r > 0))
            def _():
                relay(1, r - 1, d, side, t).start()

        for d, s in arrivals[len(parts):]:
            take_a(d, s)
        for d in range(n_row):
            for s in range(sub):
                sib_copy(d, s).wait_recv()
        own.wait()

    for d in range(n_row):
        for s in range(sub):
            sib_copy(d, s).wait_send()
            if d:
                plane_copy(d, s).wait_send()
    for d, side, t in parts:
        @pl.when((r >= k) & (r < n_row - 1))
        def _():
            relay(0, r, d, side, t).wait_send()

        @pl.when((r <= k) & (r > 0))
        def _():
            relay(1, r, d, side, t).wait_send()


def exchange(x, n_row):
    rows, cols = x.shape
    n_col = 2 * n_row
    sub = SUB if n_row <= 4 else SUB // 2
    hsub = sub // 2
    dma = pltpu.SemaphoreType.DMA
    return pl.pallas_call(
        functools.partial(exchange_kernel, n_row, sub),
        out_shape=(
            jax.ShapeDtypeStruct((rows, cols * n_col), x.dtype),
            jax.ShapeDtypeStruct((rows // 2, cols * n_col), x.dtype),
        ),
        in_specs=[pl.BlockSpec(memory_space=pltpu.VMEM)],
        out_specs=(pl.BlockSpec(memory_space=pl.ANY),) * 2,
        scratch_shapes=[
            pltpu.VMEM((rows // 2, cols * n_col), x.dtype),
            dma,
            dma((n_row, sub)),
            dma((n_row, sub)),
            dma((n_row, 2, sub)),
            dma((2, n_row, 2, hsub)),
            dma((n_row, 2, hsub)),
            dma,
        ],
        compiler_params=pltpu.CompilerParams(collective_id=0, has_side_effects=True),
        name="exchange",
    )(x)


def project_kernel(
    n_row, w_ref, g_ref, t_ref, p_ref,
    w_in, g_in, w_sum, g_sum, w_full, g_full, send_1, recv_1, send_2, recv_2,
):
    r = lax.axis_index("row")
    c = lax.axis_index("col")
    barrier = pltpu.get_barrier_semaphore()
    for d in range(1, n_row):
        pl.semaphore_signal(barrier, inc=1, device_id=(r ^ d, c), device_id_type=MESH)
    pl.semaphore_wait(barrier, n_row - 1)
    pairs = ((w_ref, w_in, w_sum, w_full), (g_ref, g_in, g_sum, g_full))

    def part(array, owner):
        size = array.shape[0] // n_row
        return pl.ds(pl.multiple_of(owner * size, size), size)

    def scatter(d, i):
        array, landing, _, _ = pairs[i]
        return pltpu.make_async_remote_copy(
            src_ref=array.at[part(array, r ^ d), :], dst_ref=landing.at[d],
            send_sem=send_1.at[d, i], recv_sem=recv_1.at[d, i],
            device_id=(r ^ d, c), device_id_type=MESH,
        )

    def spread(d, i):
        array, _, total, full = pairs[i]
        return pltpu.make_async_remote_copy(
            src_ref=total, dst_ref=full.at[part(array, r), :],
            send_sem=send_2.at[d, i], recv_sem=recv_2.at[d, i],
            device_id=(r ^ d, c), device_id_type=MESH,
        )

    every = [(d, i) for d in range(1, n_row) for i in (1, 0)]
    for d, i in every:
        scatter(d, i).start()
    for d, i in every:
        scatter(d, i).wait_recv()
    for i in (1, 0):
        array, landing, total, full = pairs[i]
        value = array[part(array, r), :]
        for d in range(1, n_row):
            value = value + landing[d]
        total[...] = value
    for i in (1, 0):
        array, _, total, full = pairs[i]
        full[part(array, r), :] = total[...]
    for d, i in every:
        spread(d, i).start()
    for d, i in every:
        spread(d, i).wait_recv()
    highest = lax.Precision.HIGHEST
    width = g_ref.shape[0]
    second = jnp.dot(
        t_ref[1], w_full[width:, :], precision=highest, preferred_element_type=jnp.float32
    ).astype(jnp.bfloat16)
    first = w_full[:width, :] - jnp.dot(
        g_full[...], second.astype(jnp.float32),
        precision=highest, preferred_element_type=jnp.float32,
    )
    first = jnp.dot(t_ref[0], first, precision=highest, preferred_element_type=jnp.float32)
    p_ref[0] = first.astype(jnp.bfloat16)
    p_ref[1] = second
    for d, i in every:
        scatter(d, i).wait_send()
        spread(d, i).wait_send()


def project(w, g, factors, n_row):
    dma = pltpu.SemaphoreType.DMA((n_row, 2))
    width, columns = g.shape[0], w.shape[1]
    vmem = pl.BlockSpec(memory_space=pltpu.VMEM)

    def landing(array):
        return pltpu.VMEM((n_row, array.shape[0] // n_row, array.shape[1]), jnp.float32)

    def total(array):
        return pltpu.VMEM((array.shape[0] // n_row, array.shape[1]), jnp.float32)

    return pl.pallas_call(
        functools.partial(project_kernel, n_row),
        out_shape=jax.ShapeDtypeStruct((2, width, columns), jnp.bfloat16),
        in_specs=[vmem] * 3,
        out_specs=vmem,
        scratch_shapes=[
            landing(w), landing(g), total(w), total(g),
            pltpu.VMEM(w.shape, jnp.float32), pltpu.VMEM(g.shape, jnp.float32),
            dma, dma, dma, dma,
        ],
        compiler_params=pltpu.CompilerParams(collective_id=1, has_side_effects=True),
        name="project",
    )(w, g, factors)


def region_kernel(index_ref, p_ref, vecs_ref, refl_ref, out_ref, vecs, refl, sems):
    count = vecs.shape[0]

    def copies(b):
        at = index_ref[b]
        return (
            pltpu.make_async_copy(vecs_ref.at[at], vecs.at[b], sems.at[b, 0]),
            pltpu.make_async_copy(refl_ref.at[0, at], refl.at[0, b], sems.at[b, 1]),
            pltpu.make_async_copy(refl_ref.at[1, at], refl.at[1, b], sems.at[b, 2]),
        )

    for b in range(count):
        for copy in copies(b):
            copy.start()
    for b in range(count):
        for copy in copies(b):
            copy.wait()
        value = vecs[b].astype(jnp.float32)
        value = value - jnp.dot(refl[1, b], p_ref[1], preferred_element_type=jnp.float32)
        value = value - jnp.dot(refl[0, b], p_ref[0], preferred_element_type=jnp.float32)
        out_ref[b] = value.astype(out_ref.dtype)


def region_rows(index, applied, vecs, refl):
    count = index.shape[0]
    columns, width = vecs.shape[2], refl.shape[3]
    vmem = pl.BlockSpec(memory_space=pltpu.VMEM)
    hbm = pl.BlockSpec(memory_space=pl.ANY)
    return pl.pallas_call(
        region_kernel,
        out_shape=jax.ShapeDtypeStruct((count, BLOCK, columns), vecs.dtype),
        in_specs=[pl.BlockSpec(memory_space=pltpu.SMEM), vmem, hbm, hbm],
        out_specs=vmem,
        scratch_shapes=[
            pltpu.VMEM((count, BLOCK, columns), vecs.dtype),
            pltpu.VMEM((2, count, BLOCK, width), refl.dtype),
            pltpu.SemaphoreType.DMA((count, 3)),
        ],
        name="region",
    )(index, applied, vecs, refl)


def per_device(n_row, eigvecs, reflectors, factors, frequencies, region_blocks):
    columns = eigvecs.shape[1]
    width = reflectors.shape[2]
    local = lax.dot_general(
        reflectors, eigvecs, (((1,), (0,)), ((), ())), preferred_element_type=jnp.float32
    ).reshape(2 * width, columns)
    cross_local = contract_rows(reflectors[0], reflectors[1])
    applied = project(local, cross_local, jnp.triu(factors), n_row)
    local_blocks = eigvecs.shape[0] // BLOCK
    local_index = region_blocks - lax.axis_index("row") * local_blocks
    region = region_rows(
        local_index,
        applied,
        eigvecs.reshape(local_blocks, BLOCK, columns),
        reflectors.reshape(2, local_blocks, BLOCK, width),
    ).reshape(-1, columns)
    weight = 1.0 / jnp.tanh(frequencies / 2.0) / (2.0 * frequencies)
    mine, partner = exchange(region, n_row)
    scaled = (mine.astype(jnp.float32) * weight[None, :]).astype(jnp.bfloat16)
    return contract_cols(scaled, partner)


def solution(mesh):
    return jax.shard_map(
        functools.partial(per_device, mesh.shape["row"]),
        mesh=mesh,
        in_specs=(P("row", "col"), P(None, "row", None), P(), P(), P("row")),
        out_specs=P("row", "col"),
        check_vma=False,
    )
```

profile of v0, /device:TPU:6, one launch (start us, length us, event | category | flops | bytes accessed | tf_op | source)
XLA Modules:
  0.0 178.1 jit_solution(3935012276134980721)
XLA Ops:
  0.0 0.0 copy-start.1
  0.0 0.0 copy-start
  0.0 1.4 broadcast_subtract_fusion.index_ref
  1.4 1.0 multiply_divide_fusion
  2.3 0.1 iota_compare_fusion
  2.4 4.1 %fusion.4.g_ref = f32[128,128]{1,0:T(8,128)} fusion(bf16[2,10240,128]{2,1,0:T(8,128)(2,1)} %param.6), kind=kOutput, calls=%fused_computation.5 | convolution fusion | flops 335544320 | bytes 5308416 | tf_op jit(solution)/shard_map/dot_general | solution.py:16
  6.5 0.0 copy-done.1
  6.5 0.7 broadcast_select_fusion.t_ref
  7.1 0.0 copy-done
  7.2 4.8 %fusion.2 = f32[2,128,256]{2,1,0:T(8,128)} fusion(bf16[2,10240,128]{2,1,0:T(8,128)(2,1)S(1)} %copy-done, bf16[10240,256]{1,0:T(8,128)(2,1)} %param.5), kind=kOutput, calls=%fused_computation.3 | convolution fusion | flops 1342177280 | bytes 10747904 | tf_op jit(solution)/shard_map/dot_general | solution.py:364
  11.9 20.8 %project.1.p_ref = bf16[2,128,256]{2,1,0:T(8,128)(2,1)} custom-call(f32[256,256]{1,0:T(8,128)} %bitcast.18, f32[128,128]{1,0:T(8,128)} %fusion.4.g_ref, f32[2,128,128]{2,1,0:T(8,128)} %broadcast_select_fusion.t_ref), custom_call_target="tpu_custom_call" | custom-call | tf_op jit(solution)/shard_map/project/pallas_call | solution.py:304
  32.8 6.5 %region.1 = bf16[18,128,256]{2,1,0:T(8,128)(2,1)} custom-call(s32[18]{0:T(128)} %broadcast_subtract_fusion.index_ref, bf16[2,128,256]{2,1,0:T(8,128)(2,1)} %project.1.p_ref, bf16[80,128,256]{2,1,0:T(8,128)(2,1)} %bitcast.16, bf16[2,80,128,128]{3,2,1,0:T(8,128)(2,1)} %bitcast.15), custom_call_target="tpu_custom_call" | custom-call | tf_op jit(solution)/shard_map/region/pallas_call | solution.py:347
  39.2 121.0 %exchange.1 = (bf16[2304,2048]{1,0:T(8,128)(2,1)}, bf16[1152,2048]{1,0:T(8,128)(2,1)}) custom-call(bf16[2304,256]{1,0:T(8,128)(2,1)} %bitcast.17), custom_call_target="tpu_custom_call" | custom-call | tf_op jit(solution)/shard_map/exchange/pallas_call | solution.py:203
  160.2 17.9 %fusion = f32[2304,1152]{1,0:T(8,128)} fusion(bf16[1152,2048]{1,0:T(8,128)(2,1)} %get-tuple-element.8, bf16[2304,2048]{1,0:T(8,128)(2,1)} %get-tuple-element.7, f32[2048]{0:T(1024)S(1)} %multiply_divide_fusion), kind=kOutput, calls=%fused_computation.1 | convolution fusion | flops 10885791744 | bytes 24780800 | tf_op jit(solution)/shard_map/dot_general | solution.py:22
  (1 shorter events, 0.0 us)
Async XLA Ops:
  0.0 6.5 %copy-start.1 = (f32[2,128,128]{2,1,0:T(8,128)S(1)}, f32[2,128,128]{2,1,0:T(8,128)}, u32[]{:S(2)}) copy-start(f32[2,128,128]{2,1,0:T(8,128)} %param.7) | copy-start | bytes 393220
  0.0 7.1 %copy-start = (bf16[2,10240,128]{2,1,0:T(8,128)(2,1)S(1)}, bf16[2,10240,128]{2,1,0:T(8,128)(2,1)}, u32[]{:S(2)}) copy-start(bf16[2,10240,128]{2,1,0:T(8,128)(2,1)} %param.6) | copy-start | bytes 15728644
where the time goes:
time: 178 us
  Pallas kernels  148 us (83%)
  matrix products  26.7 us (15%)
  other arithmetic  3.08 us (2%)
    pallas_call x1, Pallas kernels, exchange(): pl.pallas_call(functools.partial(exchange_kernel, n_row, sub), out_shape=...  121 us
    pallas_call x1, Pallas kernels, project(): pl.pallas_call(functools.partial(project_kernel, n_row), out_shape=jax.Sh...  20.8 us
    dot_general x1, matrix products, contract_cols(): lax.dot_general(left, right, (((1,), (1,)), ((), ())), preferred_element_...  17.9 us
    pallas_call x1, Pallas kernels, region_rows(): pl.pallas_call(region_kernel, out_shape=jax.ShapeDtypeStruct((count, BLOC...  6.48 us
    dot_general x1, matrix products, per_device(): lax.dot_general(reflectors, eigvecs, (((1,), (0,)), ((), ())), preferred_...  4.79 us
    dot_general x1, matrix products, contract_rows(): lax.dot_general(left, right, (((0,), (0,)), ((), ())), preferred_element_...  4.06 us

commit v1 on v0

--- a/solution.py
+++ b/solution.py
@@ -380,9 +380,684 @@
     return contract_cols(scaled, partner)
 
 
+BF = jnp.bfloat16
+F32 = jnp.float32
+HIGH = lax.Precision.HIGHEST
+
+
+def dot_nt(left, right, **kw):
+    return lax.dot_general(left, right, (((1,), (1,)), ((), ())), preferred_element_type=F32, **kw)
+
+
+def dot_tn(left, right):
+    return lax.dot_general(left, right, (((0,), (0,)), ((), ())), preferred_element_type=F32)
+
+
+def prep_kernel(chunks, index_ref, vecs_ref, refl_ref, x_ref, y_ref, w_ref, g_ref,
+                vecs, refl, w_acc, g_acc, gather_sem, vec_sem, refl_sem):
+    count = x_ref.shape[0]
+    base = lax.axis_index("row") * vecs_ref.shape[0]
+    blocks = vecs_ref.shape[0] // chunks
+
+    def gather(b):
+        at = index_ref[b] - base
+        return (
+            pltpu.make_async_copy(vecs_ref.at[at], x_ref.at[b], gather_sem.at[b, 0]),
+            pltpu.make_async_copy(refl_ref.at[0, at], y_ref.at[0, b], gather_sem.at[b, 1]),
+            pltpu.make_async_copy(refl_ref.at[1, at], y_ref.at[1, b], gather_sem.at[b, 2]),
+        )
+
+    def load(i):
+        part = pl.ds(i * blocks, blocks)
+        return (
+            pltpu.make_async_copy(vecs_ref.at[part], vecs.at[part], vec_sem.at[i]),
+            pltpu.make_async_copy(refl_ref.at[0, part], refl.at[0, part], refl_sem.at[i, 0]),
+            pltpu.make_async_copy(refl_ref.at[1, part], refl.at[1, part], refl_sem.at[i, 1]),
+        )
+
+    for i in range(chunks):
+        for copy in load(i):
+            copy.start()
+    for b in range(count):
+        for copy in gather(b):
+            copy.start()
+    rows = blocks * BLOCK
+    for i in range(chunks):
+        for copy in load(i):
+            copy.wait()
+        part = pl.ds(i * blocks, blocks)
+        e = vecs[part].reshape(rows, vecs.shape[2])
+        y0 = refl[0, part].reshape(rows, refl.shape[3])
+        y1 = refl[1, part].reshape(rows, refl.shape[3])
+        w = dot_tn(e, jnp.concatenate([y0, y1], axis=1))
+        g = dot_tn(y0, y1)
+        if i:
+            w = w + w_acc[...]
+            g = g + g_acc[...]
+        if i < chunks - 1:
+            w_acc[...] = w
+            g_acc[...] = g
+        else:
+            w_ref[...] = w.astype(BF)
+            g_ref[...] = g.astype(BF)
+    for b in range(count):
+        for copy in gather(b):
+            copy.wait()
+
+
+def prep(index, vecs, refl):
+    blocks, _, columns = vecs.shape
+    width = refl.shape[3]
+    count = index.shape[0]
+    chunks = 10
+    vmem = pl.BlockSpec(memory_space=pltpu.VMEM)
+    hbm = pl.BlockSpec(memory_space=pltpu.HBM)
+    dma = pltpu.SemaphoreType.DMA
+    return pl.pallas_call(
+        functools.partial(prep_kernel, chunks),
+        out_shape=(
+            pltpu.VMEM((count, BLOCK, columns), BF),
+            pltpu.VMEM((2, count, BLOCK, width), BF),
+            pltpu.VMEM((columns, 2 * width), BF),
+            pltpu.VMEM((width, width), BF),
+        ),
+        in_specs=[pl.BlockSpec(memory_space=pltpu.SMEM), hbm, hbm],
+        out_specs=(vmem,) * 4,
+        scratch_shapes=[
+            pltpu.VMEM(vecs.shape, BF),
+            pltpu.VMEM(refl.shape, BF),
+            pltpu.VMEM((columns, 2 * width), F32),
+            pltpu.VMEM((width, width), F32),
+            dma((count, 3)), dma((chunks,)), dma((chunks, 2)),
+        ],
+        compiler_params=pltpu.CompilerParams(vmem_limit_bytes=24 << 20),
+        name="prep",
+    )(index, vecs, refl)
+
+
+def spread_kernel(
+    x_ref, y_ref, w_ref, g_ref, t_ref, f_ref, acc_ref, sa_ref, last_ref,
+    buf, tbuf, rbuf, w_in, g_in, g_full, p_full, weight,
+    w_send, w_recv, g_send, g_recv, h_send, h_recv, p_send, p_recv,
+    own_send, relay_send, zrel_send, zsrc_send, detz_send, deti_send, rr_send,
+    ax, ay, ad, asib, zb, det, tz, rr,
+):
+    r = lax.axis_index("row")
+    c = lax.axis_index("col")
+    k = c // 2
+    h = lax.rem(c, 2)
+    o = 1 - h
+    count = x_ref.shape[0]
+    half = count // 2
+    columns = x_ref.shape[2]
+    width = g_ref.shape[0]
+    quarter = columns // 4
+    last_row = 3
+
+    def col(chip, core):
+        return 2 * chip + core
+
+    barrier = pltpu.get_barrier_semaphore()
+
+    def greet(row, column):
+        pl.semaphore_signal(barrier, inc=1, device_id=(row, column), device_id_type=MESH)
+
+    for d in range(1, 4):
+        greet(lax.rem(r + d, 4), c)
+    for d in (1, 2):
+        for core in (0, 1):
+            greet(r, col(k ^ d, core))
+    greet(r, col(k, o))
+    pl.semaphore_wait(barrier, 8)
+
+    def remote(src, dst, send, recv, row, column):
+        return pltpu.make_async_remote_copy(
+            src_ref=src, dst_ref=dst, send_sem=send, recv_sem=recv,
+            device_id=(row, column), device_id_type=MESH,
+        )
+
+    def w_copy(d):
+        q = lax.rem(r + d, 4)
+        part = pl.ds(pl.multiple_of(q * quarter, quarter), quarter)
+        return remote(w_ref.at[part], w_in.at[d], w_send.at[d], w_recv.at[d], q, c)
+
+    g_half = width // 2
+
+    def g_copy(d):
+        q = lax.rem(r + d, 4)
+        part = pl.ds(pl.multiple_of(h * g_half, g_half), g_half)
+        return remote(g_ref.at[part], g_in.at[d], g_send.at[d], g_recv.at[d], q, c)
+
+    for d in (2, 1, 3):
+        g_copy(d).start()
+        w_copy(d).start()
+
+    f = f_ref[...]
+    weight[...] = 1.0 / jnp.tanh(f / 2.0) / (2.0 * f)
+    row_at = lax.broadcasted_iota(jnp.int32, (width, width), 0)
+    col_at = lax.broadcasted_iota(jnp.int32, (width, width), 1)
+    upper = row_at <= col_at
+    zero = jnp.zeros((width, width), F32)
+    t0 = jnp.where(upper, t_ref[0], zero)
+    t1 = jnp.where(upper, t_ref[1], zero)
+
+    g_part = pl.ds(pl.multiple_of(h * g_half, g_half), g_half)
+    for d in (1, 2, 3):
+        g_copy(d).wait_recv()
+    value = g_ref[g_part, :].astype(F32)
+    for d in (1, 2, 3):
+        value = value + g_in[d].astype(F32)
+    g_full[h] = value
+    h_copy = remote(g_full.at[h], g_full.at[h], h_send, h_recv, r, col(k, o))
+    h_copy.start()
+    for d in (1, 2, 3):
+        w_copy(d).wait_recv()
+    mine = pl.ds(pl.multiple_of(r * quarter, quarter), quarter)
+    w = w_ref[mine, :].astype(F32)
+    for d in (1, 2, 3):
+        w = w + w_in[d].astype(F32)
+    second = dot_nt(w[:, width:], t1, precision=HIGH).astype(BF)
+    h_copy.wait_recv()
+    g = jnp.concatenate([g_full[0], g_full[1]], axis=0)
+    first = w[:, :width] - dot_nt(second.astype(F32), g, precision=HIGH)
+    first = dot_nt(first, t0, precision=HIGH).astype(BF)
+    p_full[r, :, :width] = first
+    p_full[r, :, width:] = second
+
+    def p_copy(d):
+        return remote(p_full.at[r], p_full.at[r], p_send.at[d], p_recv.at[d], lax.rem(r + d, 4), c)
+
+    def p_arrival(d):
+        q = lax.rem(r + d, 4)
+        return remote(p_full.at[q], p_full.at[q], p_send.at[d], p_recv.at[4 - d], q, c)
+
+    for d in (2, 1, 3):
+        p_copy(d).start()
+    for d in (1, 2, 3):
+        p_arrival(d).wait_recv()
+
+    def block_of(n):
+        return lax.rem(n, 2) * half + n // 2
+
+    def a_copy(way, n):
+        b = block_of(n)
+        src = buf.at[c, b]
+        if way == 2:
+            return remote(src, buf.at[c, b], own_send.at[2], asib.at[0, n], r, col(k, o))
+        sem = ax if way == 0 else ay
+        return remote(src, buf.at[c, b], own_send.at[way], sem.at[n], r, col(k ^ (way + 1), h))
+
+    corner = (k == 0) | (k == 3)
+    is_low = k == 0
+    rank = jnp.where(is_low, r, 3 - r)
+    away = jnp.where(is_low, -1, 1)
+    slot = jnp.where(is_low, 0, 1)
+    early = 5
+
+    def det_own(hops, n):
+        b = block_of(n)
+        return remote(
+            buf.at[c, b], tbuf.at[rank - 1, b], detz_send.at[hops - 1], tz.at[rank - 1, n],
+            r + away * hops, c,
+        )
+
+    applied = p_full[...].reshape(columns, 2 * width)
+
+    def make_region(n, _):
+        b = block_of(n)
+        y = jnp.concatenate([y_ref[0, b], y_ref[1, b]], axis=1)
+        buf[c, b] = (x_ref[b].astype(F32) - dot_nt(y, applied)).astype(BF)
+        for way in (0, 1, 2):
+            a_copy(way, n).start()
+
+        @pl.when(corner & ((rank > 1) | ((rank == 1) & (n < early))))
+        def _():
+            @pl.when(rank == 3)
+            def _():
+                det_own(2, n).start()
+
+            det_own(1, n).start()
+
+        return 0
+
+    lax.fori_loop(0, count, make_region, 0)
+
+    def a_arrival(way, n):
+        src = col(k ^ (way + 1), h)
+        b = block_of(n)
+        at = buf.at[src, b]
+        sem = (ax, ay, ad)[way]
+        return remote(at, at, own_send.at[2], sem.at[n], r, col(k, o))
+
+    def sib_copy(j, n):
+        src = col(k ^ j, h)
+        b = block_of(n)
+        at = buf.at[src, b]
+        return remote(at, at, own_send.at[2], asib.at[j, n], r, col(k, o))
+
+    def sib_arrival(j, n):
+        src = col(k ^ j, o)
+        b = block_of(n)
+        at = buf.at[src, b]
+        return remote(at, at, own_send.at[2], asib.at[j, n], r, col(k, o))
+
+    def relay(way, n):
+        src = col(k ^ (way + 1), h)
+        at = buf.at[src, block_of(n)]
+        to = k ^ (2 - way)
+        return remote(at, at, relay_send.at[way], ad.at[n], r, col(to, h))
+
+    down = r < k
+    at_source = r == k
+    step = jnp.where(down, -1, 1)
+    depth = jnp.where(down, k, 3 - k)
+
+    def z_piece(t, depth, is_down):
+        third = t // (2 * half)
+        n = lax.rem(t, 2 * half) // 2
+        e = lax.rem(t, 2)
+        j1 = jnp.where(depth == 3, 2, 3)
+        j2 = 6 - depth - j1
+        j = jnp.where(third == 0, depth, jnp.where(third == 1, j1, j2))
+        j = jnp.where(is_down, j, 3 - j)
+        return col(j, lax.rem(h + e, 2)), n
+
+    steps = 3 * 2 * half
+
+    def z_relay(t):
+        src, n = z_piece(t, depth, down)
+        at = buf.at[src, count + n]
+        return remote(at, at, zrel_send, zb.at[t], r + step, c)
+
+    def z_source(t, is_down):
+        src, n = z_piece(t, k if is_down else 3 - k, jnp.bool_(is_down))
+        return remote(
+            buf.at[src, h * half + n], buf.at[src, count + n],
+            zsrc_send.at[0 if is_down else 1], zb.at[t], r + (-1 if is_down else 1), c,
+        )
+
+    def det_z(p, n):
+        at = tbuf.at[p - 1, block_of(n)]
+        return remote(at, at, detz_send.at[p], tz.at[p - 1, n], r + away, c)
+
+    def det_plane(p, n):
+        b = block_of(n)
+        src = tbuf.at[p - 1, b]
+        core = lax.rem(n, 2)
+        if p < 3:
+            return remote(
+                src, buf.at[c, count + n // 2], deti_send.at[p], det.at[h, n // 2],
+                r, col(k ^ p, core),
+            )
+        return remote(
+            src, rbuf.at[slot, n // 2], deti_send.at[p], rr.at[slot, n // 2],
+            r, col(k ^ (1 + h), core),
+        )
+
+    between = (k == 1) | (k == 2)
+
+    def rr_copy(way, n):
+        low = k - 1 if way == 0 else 2 - k
+        src = low if way == 0 else low + 6
+        return remote(
+            rbuf.at[way, n], buf.at[src, count + n], rr_send.at[way], det.at[low, n],
+            r, col(3 if way == 0 else 0, h),
+        )
+
+    def det_arrival(low, n):
+        src = jnp.where(down, low, low + 6)
+        at = buf.at[src, count + n]
+        return remote(at, at, own_send.at[2], det.at[low, n], r, col(k, o))
+
+    mine_at = jnp.where(at_source, h * half, count)
+
+    def scale(q):
+        src = col(k ^ (q // 2), lax.rem(h + q, 2))
+        wt = jnp.concatenate([weight[pl.ds(2 * src, 1), :], weight[pl.ds(2 * src + 1, 1), :]], axis=1)
+
+        def one(b, _):
+            rows = pl.ds(pl.multiple_of(b * BLOCK, BLOCK), BLOCK)
+            sa_ref[src, rows, :] = (buf[src, b].astype(F32) * wt).astype(BF)
+            return 0
+
+        lax.fori_loop(0, count, one, 0)
+
+    tile = 256
+
+    def pair(q, tiles):
+        at = mine_at + 2 * q
+        lanes = pl.ds(pl.multiple_of(q * tile, tile), tile)
+
+        def one(i, _):
+            rows = pl.ds(pl.multiple_of(i * tile, tile), tile)
+            total = jnp.zeros((tile, tile), F32)
+            for s in range(8):
+                total = total + dot_nt(sa_ref[s, rows, :], buf[s, pl.ds(at, 2)].reshape(tile, columns))
+            acc_ref[rows, lanes] = total
+            return 0
+
+        lax.fori_loop(tiles[0], tiles[1], one, 0)
+
+    def wait_detours(n):
+        @pl.when(jnp.logical_not(at_source))
+        def _():
+            for low in (0, 1):
+                det_arrival(low, n).wait_recv()
+
+    def z_source_step(t):
+        @pl.when(at_source)
+        def _():
+            @pl.when(r > 0)
+            def _():
+                z_source(t, True).start()
+
+            @pl.when(r < last_row)
+            def _():
+                z_source(t, False).start()
+
+    hops = jnp.where(down, k - r, r - k)
+    lag = 2
+
+    def z_relay_step(u):
+        t = u - lag * hops
+
+        @pl.when(jnp.logical_not(at_source) & (t >= 0) & (t < steps))
+        def _():
+            z_relay(t).wait_recv()
+
+            @pl.when((down & (r > 0)) | (jnp.logical_not(down) & (r < last_row)))
+            def _():
+                z_relay(t).start()
+
+    def first_third(t, _):
+        @pl.when(lax.rem(t, 2) == 0)
+        def _():
+            n = t
+            sib_arrival(0, n).wait_recv()
+            sib_arrival(0, n + 1).wait_recv()
+        z_source_step(t)
+        return 0
+
+    lax.fori_loop(0, count, first_third, 0)
+
+    n_tiles = acc_ref.shape[0] // tile
+
+    def beat(u, _):
+        def span(first, length):
+            return (u >= first) & (u < first + length)
+
+        z_relay_step(u)
+
+        @pl.when(span(2, count))
+        def _():
+            n = u - 2
+            for way in (0, 1):
+                a_arrival(way, n).wait_recv()
+                sib_copy(way + 1, n).start()
+            even = lax.rem(n, 2) == 0
+
+            @pl.when(even)
+            def _():
+                relay(0, n).start()
+
+            @pl.when(jnp.logical_not(even))
+            def _():
+                relay(1, n).start()
+
+        @pl.when(span(4, count))
+        def _():
+            n = u - 4
+            sib_arrival(1, n).wait_recv()
+            sib_arrival(2, n).wait_recv()
+
+        @pl.when(span(6, count))
+        def _():
+            z_source_step(u + count - 6)
+
+        @pl.when(corner)
+        def _():
+            n5 = (u - 5) // 2
+
+            @pl.when((rank == 1) & span(5, 2 * count) & (lax.rem(u, 2) == 1))
+            def _():
+                for p in (3, 2):
+                    det_z(p, n5).wait_recv()
+                    det_z(p, n5).start()
+
+            @pl.when((rank == 1) & span(36, count - early))
+            def _():
+                det_own(1, u - 36 + early).start()
+
+            v = u - 22
+            n22 = (2 * v) // 3
+
+            @pl.when(span(22, 27) & (lax.rem(v, 3) != 1))
+            def _():
+                for p in (3, 2):
+                    @pl.when(p > rank)
+                    def _():
+                        @pl.when(rank != 1)
+                        def _():
+                            det_z(p, n22).wait_recv()
+
+                        det_plane(p, n22).start()
+
+            @pl.when((rank == 0) & (span(22, early) | span(40 + early, count - early)))
+            def _():
+                n = jnp.where(u < 40, u - 22, u - 40)
+                det_z(1, n).wait_recv()
+                det_plane(1, n).start()
+
+        w = u - 26 - 2 * h
+        @pl.when(between & (w >= 0) & (w < 3 * half) & (lax.rem(w, 3) == 0))
+        def _():
+            n = w // 3
+            for way in (0, 1):
+                @pl.when(r < last_row if way == 0 else r > 0)
+                def _():
+                    at = rbuf.at[way, n]
+                    remote(at, at, rr_send.at[way], rr.at[way, n], r, col(k, o)).wait_recv()
+                    rr_copy(way, n).start()
+
+        @pl.when(span(23, half))
+        def _():
+            for i in range(2):
+                n = 2 * (u - 23) + i
+                a_arrival(2, n).wait_recv()
+                sib_copy(3, n).start()
+
+        @pl.when(span(25, half))
+        def _():
+            for i in range(2):
+                sib_arrival(3, 2 * (u - 25) + i).wait_recv()
+
+        @pl.when(span(27, count))
+        def _():
+            z_source_step(u + 2 * count - 27)
+
+        @pl.when(span(34, 8))
+        def _():
+            scale(u - 34)
+
+        q = (u - 46) // 4
+        i = lax.rem(u - 46, 4)
+
+        @pl.when(span(46, 12) & (i == 0))
+        def _():
+            wait_detours(2 * q)
+            wait_detours(2 * q + 1)
+
+        @pl.when(span(46, 12) & (i < 3))
+        def _():
+            pair(q, (i * (n_tiles // 3), (i + 1) * (n_tiles // 3)))
+
+        return 0
+
+    lax.fori_loop(0, steps + 3 * lag, beat, 0)
+    wait_detours(6)
+    wait_detours(7)
+    pair(3, (0, n_tiles))
+    wait_detours(8)
+    for s in range(8):
+        last_ref[s] = buf[s, mine_at + 8]
+
+    def drain(ref, sem):
+        pltpu.make_async_copy(ref, ref, sem).wait()
+
+    for d in (1, 2, 3):
+        w_copy(d).wait_send()
+        g_copy(d).wait_send()
+        p_copy(d).wait_send()
+    h_copy.wait_send()
+    shard = buf.at[0, pl.ds(0, count)]
+    for way in (0, 1):
+        drain(shard, own_send.at[way])
+        drain(buf.at[0, pl.ds(0, half)], relay_send.at[way])
+    drain(buf.at[:, pl.ds(0, half)], own_send.at[2])
+
+    @pl.when(at_source)
+    def _():
+        @pl.when(r > 0)
+        def _():
+            drain(buf.at[pl.ds(0, 2)], zsrc_send.at[0])
+
+        @pl.when(r < last_row)
+        def _():
+            drain(buf.at[pl.ds(0, 2)], zsrc_send.at[1])
+
+    @pl.when((down & (r > 0)) | ((r > k) & (r < last_row)))
+    def _():
+        drain(buf.at[pl.ds(0, 2)], zrel_send)
+
+    @pl.when(corner)
+    def _():
+        for p in (3, 2, 1):
+            @pl.when(p > rank)
+            def _():
+                drain(shard, deti_send.at[p])
+
+        @pl.when(rank == 1)
+        def _():
+            for p in (3, 2):
+                drain(shard, detz_send.at[p])
+
+        @pl.when(rank > 0)
+        def _():
+            drain(shard, detz_send.at[0])
+
+        @pl.when(rank == 3)
+        def _():
+            drain(shard, detz_send.at[1])
+
+    @pl.when(between)
+    def _():
+        for way in (0, 1):
+            @pl.when(r < last_row if way == 0 else r > 0)
+            def _():
+                drain(rbuf.at[0], rr_send.at[way])
+
+
+def spread(x, y, w, g, factors, frequencies):
+    count, _, columns = x.shape
+    width = g.shape[0]
+    half = count // 2
+    dma = pltpu.SemaphoreType.DMA
+    vmem = pl.BlockSpec(memory_space=pltpu.VMEM)
+    return pl.pallas_call(
+        spread_kernel,
+        out_shape=(
+            pltpu.VMEM((count * BLOCK, half * BLOCK), F32),
+            pltpu.VMEM((8, count * BLOCK, columns), BF),
+            pltpu.VMEM((8, BLOCK, columns), BF),
+        ),
+        in_specs=[vmem] * 6,
+        out_specs=(vmem,) * 3,
+        scratch_shapes=[
+            pltpu.VMEM((8, count + half, BLOCK, columns), BF),
+            pltpu.VMEM((3, count, BLOCK, columns), BF),
+            pltpu.VMEM((2, half, BLOCK, columns), BF),
+            pltpu.VMEM((4, columns // 4, 2 * width), BF),
+            pltpu.VMEM((4, width // 2, width), BF),
+            pltpu.VMEM((2, width // 2, width), F32),
+            pltpu.VMEM((4, columns // 4, 2 * width), BF),
+            pltpu.VMEM(frequencies.shape, F32),
+            dma((4,)), dma((4,)), dma((4,)), dma((4,)), dma, dma, dma((4,)), dma((4,)),
+            dma((3,)), dma((2,)), dma, dma((2,)), dma((4,)), dma((4,)), dma((2,)),
+            dma((count,)), dma((count,)), dma((count,)), dma((4, count)),
+            dma((3 * count,)), dma((2, half)), dma((3, count)), dma((2, half)),
+        ],
+        compiler_params=pltpu.CompilerParams(
+            collective_id=2, has_side_effects=True, vmem_limit_bytes=30 << 20
+        ),
+        name="spread",
+    )(x, y, w, g, factors, frequencies)
+
+
+def finish_kernel(acc_ref, sa_ref, last_ref, out_ref, tail, sem, tail_sem):
+    rows, columns = acc_ref.shape
+    lane = last_ref.shape[1]
+    parts = 4
+    size = rows // parts
+    done = columns - lane
+
+    def main_copy(i):
+        at = pl.ds(i * size, size)
+        return pltpu.make_async_copy(
+            acc_ref.at[at, pl.ds(0, done)], out_ref.at[at, pl.ds(0, done)], sem.at[i]
+        )
+
+    def tail_copy(i):
+        at = pl.ds(i * size, size)
+        return pltpu.make_async_copy(tail.at[at], out_ref.at[at, pl.ds(done, lane)], tail_sem.at[i])
+
+    for i in range(parts):
+        main_copy(i).start()
+    for i in range(parts):
+        at = pl.ds(i * size, size)
+        total = jnp.zeros((size, lane), F32)
+        for s in range(8):
+            total = total + dot_nt(sa_ref[s, at, :], last_ref[s])
+        tail[at] = total
+        tail_copy(i).start()
+    for i in range(parts):
+        main_copy(i).wait()
+        tail_copy(i).wait()
+
+
+def finish(acc, sa, last):
+    vmem = pl.BlockSpec(memory_space=pltpu.VMEM)
+    dma = pltpu.SemaphoreType.DMA
+    return pl.pallas_call(
+        finish_kernel,
+        out_shape=jax.ShapeDtypeStruct(acc.shape, F32),
+        in_specs=[vmem] * 3,
+        out_specs=pl.BlockSpec(memory_space=pl.ANY),
+        scratch_shapes=[pltpu.VMEM((acc.shape[0], last.shape[1]), F32), dma((4,)), dma((4,))],
+        compiler_params=pltpu.CompilerParams(vmem_limit_bytes=8 << 20),
+        name="finish",
+    )(acc, sa, last)
+
+
+def per_device_square(eigvecs, reflectors, factors, frequencies, region_blocks):
+    local_blocks = eigvecs.shape[0] // BLOCK
+    in_hbm = functools.partial(pltpu.with_memory_space_constraint, memory_space=pltpu.HBM)
+    x, y, w, g = prep(
+        region_blocks,
+        in_hbm(eigvecs.reshape(local_blocks, BLOCK, eigvecs.shape[1])),
+        in_hbm(reflectors.reshape(2, local_blocks, BLOCK, reflectors.shape[2])),
+    )
+    acc, sa, last = spread(x, y, w, g, factors, frequencies.reshape(-1, 128))
+    return finish(acc, sa, last)
+
+
 def solution(mesh):
+    shape = mesh.shape
+    if shape["row"] == 4 and shape["col"] == 8:
+        body = per_device_square
+    else:
+        body = functools.partial(per_device, shape["row"])
     return jax.shard_map(
-        functools.partial(per_device, mesh.shape["row"]),
+        body,
         mesh=mesh,
         in_specs=(P("row", "col"), P(None, "row", None), P(), P(), P("row")),
         out_specs=P("row", "col"),

time: 178 us -> 125 us (0.70)
  matrix products: 26.7 us -> 0 us
  Pallas kernels: 148 us -> 124 us
  other arithmetic: 3.08 us -> 0 us
    dot_general x3 -> x0, matrix products: 26.7 us -> none  [the longest x1 17.9 us: contract_cols(): lax.dot_general(left, right, (((1,), (1,)), ((), ())), preferred_element_...]
    pallas_call x3, Pallas kernels: 148 us -> 124 us  [the longest x1 111 us: spread(): pl.pallas_call(spread_kernel, out_shape=(pltpu.VMEM((count * BLOCK, half...]
where the time goes in v1:
time: 125 us
  Pallas kernels  124 us (99%)
    pallas_call x1, Pallas kernels, spread(): pl.pallas_call(spread_kernel, out_shape=(pltpu.VMEM((count * BLOCK, half...  111 us
    pallas_call x1, Pallas kernels, prep(): pl.pallas_call(functools.partial(prep_kernel, chunks), out_shape=(pltpu.V...  9.32 us
    pallas_call x1, Pallas kernels, finish(): pl.pallas_call(finish_kernel, out_shape=jax.ShapeDtypeStruct(acc.shape, F...  4.03 us

profile of v1, /device:TPU:6, one launch (start us, length us, event | category | flops | bytes accessed | tf_op | source)
XLA Modules:
  0.0 124.8 jit_solution(142321189758602570)
XLA Ops:
  0.0 0.0 copy-start.2
  0.0 0.7 copy-done.2
  0.7 0.0 copy-start
  0.7 0.0 copy-start.1
  0.7 9.3 %prep.1 = (bf16[18,128,256]{2,1,0:T(8,128)(2,1)S(1)}, bf16[2,18,128,128]{3,2,1,0:T(8,128)(2,1)S(1)}, bf16[256,256]{1,0:T(8,128)(2,1)S(1)}, bf16[128,128]{1,0:T(8,128)(2,1)S(1)}) custom-call(s32[18]{0:T(128)S(1)} %copy-done.2, bf16[80,128,256]{2,1,0:T(8,128)(2,1)} %bitcast.4, bf16[2,80,128,128]{3,2,1,0:T(8,128)(2,1)} %bitcast.5), custom_call_target="tpu_custom_call" | custom-call | tf_op jit(solution)/shard_map/prep/pallas_call | solution.py:456
  10.0 0.0 copy-done
  10.0 0.0 copy-done.1
  10.0 110.7 %spread.1 = (f32[2304,1152]{1,0:T(8,128)S(1)}, bf16[8,2304,256]{2,1,0:T(8,128)(2,1)S(1)}, bf16[8,128,256]{2,1,0:T(8,128)(2,1)S(1)}) custom-call(bf16[18,128,256]{2,1,0:T(8,128)(2,1)S(1)} %get-tuple-element.12.x_ref, bf16[2,18,128,128]{3,2,1,0:T(8,128)(2,1)S(1)} %get-tuple-element.13.y_ref, bf16[256,256]{1,0:T(8,128)(2,1)S(1)} %get-tuple-element.14.w_ref, ...), custom_call_target="tpu_custom_call" | custom-call | tf_op jit(solution)/shard_map/spread/pallas_call | solution.py:966
  120.7 4.0 %finish.1 = f32[2304,1152]{1,0:T(8,128)} custom-call(f32[2304,1152]{1,0:T(8,128)S(1)} %get-tuple-element.16.acc_ref, bf16[8,2304,256]{2,1,0:T(8,128)(2,1)S(1)} %get-tuple-element.17.sa_ref, bf16[8,128,256]{2,1,0:T(8,128)(2,1)S(1)} %get-tuple-element.18.last_ref), custom_call_target="tpu_custom_call" | custom-call | tf_op jit(solution)/shard_map/finish/pallas_call | solution.py:1030
Async XLA Ops:
  0.0 0.7 copy-start.2
  0.7 9.3 %copy-start = (f32[2,128,128]{2,1,0:T(8,128)S(1)}, f32[2,128,128]{2,1,0:T(8,128)}, u32[]{:S(2)}) copy-start(f32[2,128,128]{2,1,0:T(8,128)} %t_ref.1) | copy-start | bytes 393220
  0.7 9.3 %copy-start.1 = (f32[2048]{0:T(1024)S(1)}, f32[2048]{0:T(1024)}, u32[]{:S(2)}) copy-start(f32[2048]{0:T(1024)} %param.8) | copy-start | bytes 24580

commit v2 on v1

--- a/solution.py
+++ b/solution.py
@@ -393,91 +393,9 @@
     return lax.dot_general(left, right, (((0,), (0,)), ((), ())), preferred_element_type=F32)
 
 
-def prep_kernel(chunks, index_ref, vecs_ref, refl_ref, x_ref, y_ref, w_ref, g_ref,
-                vecs, refl, w_acc, g_acc, gather_sem, vec_sem, refl_sem):
-    count = x_ref.shape[0]
-    base = lax.axis_index("row") * vecs_ref.shape[0]
-    blocks = vecs_ref.shape[0] // chunks
-
-    def gather(b):
-        at = index_ref[b] - base
-        return (
-            pltpu.make_async_copy(vecs_ref.at[at], x_ref.at[b], gather_sem.at[b, 0]),
-            pltpu.make_async_copy(refl_ref.at[0, at], y_ref.at[0, b], gather_sem.at[b, 1]),
-            pltpu.make_async_copy(refl_ref.at[1, at], y_ref.at[1, b], gather_sem.at[b, 2]),
-        )
-
-    def load(i):
-        part = pl.ds(i * blocks, blocks)
-        return (
-            pltpu.make_async_copy(vecs_ref.at[part], vecs.at[part], vec_sem.at[i]),
-            pltpu.make_async_copy(refl_ref.at[0, part], refl.at[0, part], refl_sem.at[i, 0]),
-            pltpu.make_async_copy(refl_ref.at[1, part], refl.at[1, part], refl_sem.at[i, 1]),
-        )
-
-    for i in range(chunks):
-        for copy in load(i):
-            copy.start()
-    for b in range(count):
-        for copy in gather(b):
-            copy.start()
-    rows = blocks * BLOCK
-    for i in range(chunks):
-        for copy in load(i):
-            copy.wait()
-        part = pl.ds(i * blocks, blocks)
-        e = vecs[part].reshape(rows, vecs.shape[2])
-        y0 = refl[0, part].reshape(rows, refl.shape[3])
-        y1 = refl[1, part].reshape(rows, refl.shape[3])
-        w = dot_tn(e, jnp.concatenate([y0, y1], axis=1))
-        g = dot_tn(y0, y1)
-        if i:
-            w = w + w_acc[...]
-            g = g + g_acc[...]
-        if i < chunks - 1:
-            w_acc[...] = w
-            g_acc[...] = g
-        else:
-            w_ref[...] = w.astype(BF)
-            g_ref[...] = g.astype(BF)
-    for b in range(count):
-        for copy in gather(b):
-            copy.wait()
-
-
-def prep(index, vecs, refl):
-    blocks, _, columns = vecs.shape
-    width = refl.shape[3]
-    count = index.shape[0]
-    chunks = 10
-    vmem = pl.BlockSpec(memory_space=pltpu.VMEM)
-    hbm = pl.BlockSpec(memory_space=pltpu.HBM)
-    dma = pltpu.SemaphoreType.DMA
-    return pl.pallas_call(
-        functools.partial(prep_kernel, chunks),
-        out_shape=(
-            pltpu.VMEM((count, BLOCK, columns), BF),
-            pltpu.VMEM((2, count, BLOCK, width), BF),
-            pltpu.VMEM((columns, 2 * width), BF),
-            pltpu.VMEM((width, width), BF),
-        ),
-        in_specs=[pl.BlockSpec(memory_space=pltpu.SMEM), hbm, hbm],
-        out_specs=(vmem,) * 4,
-        scratch_shapes=[
-            pltpu.VMEM(vecs.shape, BF),
-            pltpu.VMEM(refl.shape, BF),
-            pltpu.VMEM((columns, 2 * width), F32),
-            pltpu.VMEM((width, width), F32),
-            dma((count, 3)), dma((chunks,)), dma((chunks, 2)),
-        ],
-        compiler_params=pltpu.CompilerParams(vmem_limit_bytes=24 << 20),
-        name="prep",
-    )(index, vecs, refl)
-
-
 def spread_kernel(
-    x_ref, y_ref, w_ref, g_ref, t_ref, f_ref, acc_ref, sa_ref, last_ref,
-    buf, tbuf, rbuf, w_in, g_in, g_full, p_full, weight,
+    chunks, index_ref, vecs_ref, refl_ref, t_ref, f_ref, acc_ref, sa_ref, last_ref,
+    index, vecs, refl, w_sum, g_sum, w_ref, g_ref, index_sem, vec_sem, refl_sem, buf, tbuf, rbuf, w_in, g_in, g_full, p_full, weight,
     w_send, w_recv, g_send, g_recv, h_send, h_recv, p_send, p_recv,
     own_send, relay_send, zrel_send, zsrc_send, detz_send, deti_send, rr_send,
     ax, ay, ad, asib, zb, det, tz, rr,
@@ -487,10 +405,11 @@
     k = c // 2
     h = lax.rem(c, 2)
     o = 1 - h
-    count = x_ref.shape[0]
+    count = index.shape[0]
     half = count // 2
-    columns = x_ref.shape[2]
-    width = g_ref.shape[0]
+    columns = vecs.shape[2]
+    width = refl.shape[3]
+    blocks = vecs.shape[0] // chunks
     quarter = columns // 4
     last_row = 3
 
@@ -508,6 +427,43 @@
         for core in (0, 1):
             greet(r, col(k ^ d, core))
     greet(r, col(k, o))
+
+    def load(i):
+        part = pl.ds(i * blocks, blocks)
+        return (
+            pltpu.make_async_copy(vecs_ref.at[part], vecs.at[part], vec_sem.at[i]),
+            pltpu.make_async_copy(refl_ref.at[0, part], refl.at[0, part], refl_sem.at[i, 0]),
+            pltpu.make_async_copy(refl_ref.at[1, part], refl.at[1, part], refl_sem.at[i, 1]),
+        )
+
+    ahead = 3
+    for i in range(ahead):
+        for copy in load(i):
+            copy.start()
+    index_copy = pltpu.make_async_copy(index_ref, index, index_sem)
+    index_copy.start()
+    rows = blocks * BLOCK
+    for i in range(chunks):
+        if i + ahead < chunks:
+            for copy in load(i + ahead):
+                copy.start()
+        for copy in load(i):
+            copy.wait()
+        part = pl.ds(i * blocks, blocks)
+        e = vecs[part].reshape(rows, columns)
+        y0 = refl[0, part].reshape(rows, width)
+        y1 = refl[1, part].reshape(rows, width)
+        w = dot_tn(e, jnp.concatenate([y0, y1], axis=1))
+        g = dot_tn(y0, y1)
+        if i:
+            w = w + w_sum[...]
+            g = g + g_sum[...]
+        w_sum[...] = w
+        g_sum[...] = g
+    w_ref[...] = w.astype(BF)
+    g_ref[...] = g.astype(BF)
+    index_copy.wait()
+
     pl.semaphore_wait(barrier, 8)
 
     def remote(src, dst, send, recv, row, column):
@@ -544,7 +500,7 @@
     g_part = pl.ds(pl.multiple_of(h * g_half, g_half), g_half)
     for d in (1, 2, 3):
         g_copy(d).wait_recv()
-    value = g_ref[g_part, :].astype(F32)
+    value = g_sum[g_part, :]
     for d in (1, 2, 3):
         value = value + g_in[d].astype(F32)
     g_full[h] = value
@@ -553,7 +509,7 @@
     for d in (1, 2, 3):
         w_copy(d).wait_recv()
     mine = pl.ds(pl.multiple_of(r * quarter, quarter), quarter)
-    w = w_ref[mine, :].astype(F32)
+    w = w_sum[mine, :]
     for d in (1, 2, 3):
         w = w + w_in[d].astype(F32)
     second = dot_nt(w[:, width:], t1, precision=HIGH).astype(BF)
@@ -601,12 +557,55 @@
             r + away * hops, c,
         )
 
+    down = r < k
+    at_source = r == k
+    step = jnp.where(down, -1, 1)
+    depth = jnp.where(down, k, 3 - k)
+
+    def z_piece(t, depth, is_down):
+        third = t // (2 * half)
+        n = jnp.where(third == 0, lax.rem(t, half), lax.rem(t, 2 * half) // 2)
+        e = jnp.where(third == 0, t // half, lax.rem(t, 2))
+        j1 = jnp.where(depth == 3, 2, 3)
+        j2 = 6 - depth - j1
+        j = jnp.where(third == 0, depth, jnp.where(third == 1, j1, j2))
+        j = jnp.where(is_down, j, 3 - j)
+        return col(j, lax.rem(h + e, 2)), n
+
+    steps = 3 * 2 * half
+
+    def z_relay(t):
+        src, n = z_piece(t, depth, down)
+        at = buf.at[src, count + n]
+        return remote(at, at, zrel_send, zb.at[t], r + step, c)
+
+    def z_source(t, is_down):
+        src, n = z_piece(t, k if is_down else 3 - k, jnp.bool_(is_down))
+        return remote(
+            buf.at[src, h * half + n], buf.at[src, count + n],
+            zsrc_send.at[0 if is_down else 1], zb.at[t], r + (-1 if is_down else 1), c,
+        )
+
+    def z_source_step(t):
+        @pl.when(at_source)
+        def _():
+            @pl.when(r > 0)
+            def _():
+                z_source(t, True).start()
+
+            @pl.when(r < last_row)
+            def _():
+                z_source(t, False).start()
+
     applied = p_full[...].reshape(columns, 2 * width)
+
+    base = r * vecs.shape[0]
 
     def make_region(n, _):
         b = block_of(n)
-        y = jnp.concatenate([y_ref[0, b], y_ref[1, b]], axis=1)
-        buf[c, b] = (x_ref[b].astype(F32) - dot_nt(y, applied)).astype(BF)
+        at = jnp.clip(index[b] - base, 0, vecs.shape[0] - 1)
+        y = jnp.concatenate([refl[0, at], refl[1, at]], axis=1)
+        buf[c, b] = (vecs[at].astype(F32) - dot_nt(y, applied)).astype(BF)
         for way in (0, 1, 2):
             a_copy(way, n).start()
 
@@ -617,6 +616,10 @@
                 det_own(2, n).start()
 
             det_own(1, n).start()
+
+        @pl.when(lax.rem(n, 2) == h)
+        def _():
+            z_source_step(n // 2)
 
         return 0
 
@@ -646,35 +649,6 @@
         at = buf.at[src, block_of(n)]
         to = k ^ (2 - way)
         return remote(at, at, relay_send.at[way], ad.at[n], r, col(to, h))
-
-    down = r < k
-    at_source = r == k
-    step = jnp.where(down, -1, 1)
-    depth = jnp.where(down, k, 3 - k)
-
-    def z_piece(t, depth, is_down):
-        third = t // (2 * half)
-        n = lax.rem(t, 2 * half) // 2
-        e = lax.rem(t, 2)
-        j1 = jnp.where(depth == 3, 2, 3)
-        j2 = 6 - depth - j1
-        j = jnp.where(third == 0, depth, jnp.where(third == 1, j1, j2))
-        j = jnp.where(is_down, j, 3 - j)
-        return col(j, lax.rem(h + e, 2)), n
-
-    steps = 3 * 2 * half
-
-    def z_relay(t):
-        src, n = z_piece(t, depth, down)
-        at = buf.at[src, count + n]
-        return remote(at, at, zrel_send, zb.at[t], r + step, c)
-
-    def z_source(t, is_down):
-        src, n = z_piece(t, k if is_down else 3 - k, jnp.bool_(is_down))
-        return remote(
-            buf.at[src, h * half + n], buf.at[src, count + n],
-            zsrc_send.at[0 if is_down else 1], zb.at[t], r + (-1 if is_down else 1), c,
-        )
 
     def det_z(p, n):
         at = tbuf.at[p - 1, block_of(n)]
@@ -711,32 +685,53 @@
 
     mine_at = jnp.where(at_source, h * half, count)
 
-    def scale(q):
-        src = col(k ^ (q // 2), lax.rem(h + q, 2))
+    from_low = jnp.logical_not(down | (at_source & (k >= 2)))
+    deep = jnp.where(from_low, 3 - k, k)
+    mid = jnp.where(deep == 3, 2, 3)
+    order = []
+    for j in (deep, mid, 6 - deep - mid, 0):
+        j = jnp.where(from_low, 3 - j, j)
+        order += [col(j, 0), col(j, 1)]
+
+    def at_place(s):
+        src = order[0]
+        for i in range(1, 8):
+            src = jnp.where(s == i, order[i], src)
+        return src
+
+    def scale(s, part):
+        src = at_place(s)
         wt = jnp.concatenate([weight[pl.ds(2 * src, 1), :], weight[pl.ds(2 * src + 1, 1), :]], axis=1)
 
-        def one(b, _):
+        def one(i, _):
+            b = part * half + i
             rows = pl.ds(pl.multiple_of(b * BLOCK, BLOCK), BLOCK)
-            sa_ref[src, rows, :] = (buf[src, b].astype(F32) * wt).astype(BF)
+            sa_ref[s, rows, :] = (buf[src, b].astype(F32) * wt).astype(BF)
             return 0
 
-        lax.fori_loop(0, count, one, 0)
+        lax.fori_loop(0, half, one, 0)
 
     tile = 256
 
-    def pair(q, tiles):
-        at = mine_at + 2 * q
-        lanes = pl.ds(pl.multiple_of(q * tile, tile), tile)
+    def product(block, lane, size, third, places, add):
+        at = mine_at + block
+        lanes = pl.ds(pl.multiple_of(lane, BLOCK), size * BLOCK)
 
         def one(i, _):
             rows = pl.ds(pl.multiple_of(i * tile, tile), tile)
-            total = jnp.zeros((tile, tile), F32)
-            for s in range(8):
-                total = total + dot_nt(sa_ref[s, rows, :], buf[s, pl.ds(at, 2)].reshape(tile, columns))
+            total = jnp.zeros((tile, size * BLOCK), F32)
+            for s in places:
+                right = buf[order[s], pl.ds(at, size)].reshape(size * BLOCK, columns)
+                total = total + dot_nt(sa_ref[s, rows, :], right)
+            if add:
+                total = total + acc_ref[rows, lanes]
             acc_ref[rows, lanes] = total
             return 0
 
-        lax.fori_loop(tiles[0], tiles[1], one, 0)
+        lax.fori_loop(third * (n_tiles // 3), (third + 1) * (n_tiles // 3), one, 0)
+
+    def pair(q, third, places, add):
+        product(2 * q, q * tile, 2, third, places, add)
 
     def wait_detours(n):
         @pl.when(jnp.logical_not(at_source))
@@ -744,17 +739,6 @@
             for low in (0, 1):
                 det_arrival(low, n).wait_recv()
 
-    def z_source_step(t):
-        @pl.when(at_source)
-        def _():
-            @pl.when(r > 0)
-            def _():
-                z_source(t, True).start()
-
-            @pl.when(r < last_row)
-            def _():
-                z_source(t, False).start()
-
     hops = jnp.where(down, k - r, r - k)
     lag = 2
 
@@ -769,16 +753,13 @@
             def _():
                 z_relay(t).start()
 
-    def first_third(t, _):
-        @pl.when(lax.rem(t, 2) == 0)
-        def _():
-            n = t
-            sib_arrival(0, n).wait_recv()
-            sib_arrival(0, n + 1).wait_recv()
-        z_source_step(t)
+    def first_third(n, _):
+        sib_arrival(0, 2 * n).wait_recv()
+        sib_arrival(0, 2 * n + 1).wait_recv()
+        z_source_step(half + n)
         return 0
 
-    lax.fori_loop(0, count, first_third, 0)
+    lax.fori_loop(0, half, first_third, 0)
 
     n_tiles = acc_ref.shape[0] // tile
 
@@ -875,13 +856,23 @@
         def _():
             z_source_step(u + 2 * count - 27)
 
-        @pl.when(span(34, 8))
-        def _():
-            scale(u - 34)
+        for first, length, place in ((6, 4, 0), (22, 4, 2), (34, 8, 4)):
+            @pl.when(span(first, length))
+            def _():
+                scale(place + (u - first) // 2, lax.rem(u - first, 2))
+
+        for first, q in ((27, 0), (31, 1), (42, 2)):
+            @pl.when(span(first, 3))
+            def _():
+                pair(q, u - first, range(4), False)
 
         q = (u - 46) // 4
         i = lax.rem(u - 46, 4)
 
+        @pl.when((u == 45) | (u == 49) | (u == 53))
+        def _():
+            pair(3, (u - 45) // 4, range(4), False)
+
         @pl.when(span(46, 12) & (i == 0))
         def _():
             wait_detours(2 * q)
@@ -889,17 +880,20 @@
 
         @pl.when(span(46, 12) & (i < 3))
         def _():
-            pair(q, (i * (n_tiles // 3), (i + 1) * (n_tiles // 3)))
+            pair(q, i, range(4, 8), True)
+
+        @pl.when(span(57, 3))
+        def _():
+            product(8, 4 * tile, 1, u - 57, range(4), False)
 
         return 0
 
     lax.fori_loop(0, steps + 3 * lag, beat, 0)
     wait_detours(6)
     wait_detours(7)
-    pair(3, (0, n_tiles))
     wait_detours(8)
-    for s in range(8):
-        last_ref[s] = buf[s, mine_at + 8]
+    for s in range(4):
+        last_ref[s] = buf[order[4 + s], pl.ds(mine_at + 6, 3)]
 
     def drain(ref, sem):
         pltpu.make_async_copy(ref, ref, sem).wait()
@@ -957,22 +951,32 @@
                 drain(rbuf.at[0], rr_send.at[way])
 
 
-def spread(x, y, w, g, factors, frequencies):
-    count, _, columns = x.shape
-    width = g.shape[0]
+def spread(index, vecs, refl, factors, frequencies):
+    count = index.shape[0]
+    columns, width = vecs.shape[2], refl.shape[3]
+    chunks = 10
     half = count // 2
     dma = pltpu.SemaphoreType.DMA
     vmem = pl.BlockSpec(memory_space=pltpu.VMEM)
+    hbm = pl.BlockSpec(memory_space=pltpu.HBM)
     return pl.pallas_call(
-        spread_kernel,
+        functools.partial(spread_kernel, chunks),
         out_shape=(
             pltpu.VMEM((count * BLOCK, half * BLOCK), F32),
             pltpu.VMEM((8, count * BLOCK, columns), BF),
-            pltpu.VMEM((8, BLOCK, columns), BF),
+            pltpu.VMEM((4, 3, BLOCK, columns), BF),
         ),
-        in_specs=[vmem] * 6,
+        in_specs=[hbm] * 3 + [vmem] * 2,
         out_specs=(vmem,) * 3,
         scratch_shapes=[
+            pltpu.SMEM((count,), jnp.int32),
+            pltpu.VMEM(vecs.shape, BF),
+            pltpu.VMEM(refl.shape, BF),
+            pltpu.VMEM((columns, 2 * width), F32),
+            pltpu.VMEM((width, width), F32),
+            pltpu.VMEM((columns, 2 * width), BF),
+            pltpu.VMEM((width, width), BF),
+            dma, dma((chunks,)), dma((chunks, 2)),
             pltpu.VMEM((8, count + half, BLOCK, columns), BF),
             pltpu.VMEM((3, count, BLOCK, columns), BF),
             pltpu.VMEM((2, half, BLOCK, columns), BF),
@@ -987,41 +991,52 @@
             dma((3 * count,)), dma((2, half)), dma((3, count)), dma((2, half)),
         ],
         compiler_params=pltpu.CompilerParams(
-            collective_id=2, has_side_effects=True, vmem_limit_bytes=30 << 20
+            collective_id=2, has_side_effects=True, vmem_limit_bytes=36 << 20
         ),
         name="spread",
-    )(x, y, w, g, factors, frequencies)
-
-
-def finish_kernel(acc_ref, sa_ref, last_ref, out_ref, tail, sem, tail_sem):
+    )(index, vecs, refl, factors, frequencies)
+
+
+def finish_kernel(acc_ref, sa_ref, last_ref, out_ref, tail, sem, pair_sem, single_sem):
     rows, columns = acc_ref.shape
-    lane = last_ref.shape[1]
+    held, blocks, lane, depth = last_ref.shape
     parts = 4
     size = rows // parts
-    done = columns - lane
+    done = columns - blocks * lane
+
+    def at(i):
+        return pl.ds(i * size, size)
 
     def main_copy(i):
-        at = pl.ds(i * size, size)
+        lanes = pl.ds(0, done)
+        return pltpu.make_async_copy(acc_ref.at[at(i), lanes], out_ref.at[at(i), lanes], sem.at[i])
+
+    def pair_copy(i):
         return pltpu.make_async_copy(
-            acc_ref.at[at, pl.ds(0, done)], out_ref.at[at, pl.ds(0, done)], sem.at[i]
-        )
-
-    def tail_copy(i):
-        at = pl.ds(i * size, size)
-        return pltpu.make_async_copy(tail.at[at], out_ref.at[at, pl.ds(done, lane)], tail_sem.at[i])
+            tail.at[at(i), pl.ds(0, 2 * lane)], out_ref.at[at(i), pl.ds(done, 2 * lane)], pair_sem.at[i]
+        )
+
+    def single_copy(i):
+        return pltpu.make_async_copy(
+            tail.at[at(i), pl.ds(2 * lane, lane)],
+            out_ref.at[at(i), pl.ds(columns - lane, lane)], single_sem.at[i],
+        )
 
     for i in range(parts):
         main_copy(i).start()
-    for i in range(parts):
-        at = pl.ds(i * size, size)
-        total = jnp.zeros((size, lane), F32)
-        for s in range(8):
-            total = total + dot_nt(sa_ref[s, at, :], last_ref[s])
-        tail[at] = total
-        tail_copy(i).start()
+    for first, count, copy in ((0, 2, pair_copy), (2, 1, single_copy)):
+        lanes = pl.ds(first * lane, count * lane)
+        for i in range(parts):
+            total = acc_ref[at(i), pl.ds(done + first * lane, count * lane)]
+            for s in range(held):
+                right = last_ref[s, first:first + count].reshape(count * lane, depth)
+                total = total + dot_nt(sa_ref[held + s, at(i), :], right)
+            tail[at(i), lanes] = total
+            copy(i).start()
     for i in range(parts):
         main_copy(i).wait()
-        tail_copy(i).wait()
+        pair_copy(i).wait()
+        single_copy(i).wait()
 
 
 def finish(acc, sa, last):
@@ -1032,7 +1047,7 @@
         out_shape=jax.ShapeDtypeStruct(acc.shape, F32),
         in_specs=[vmem] * 3,
         out_specs=pl.BlockSpec(memory_space=pl.ANY),
-        scratch_shapes=[pltpu.VMEM((acc.shape[0], last.shape[1]), F32), dma((4,)), dma((4,))],
+        scratch_shapes=[pltpu.VMEM((acc.shape[0], last.shape[1] * last.shape[2]), F32), dma((4,)), dma((4,)), dma((4,))],
         compiler_params=pltpu.CompilerParams(vmem_limit_bytes=8 << 20),
         name="finish",
     )(acc, sa, last)
@@ -1041,12 +1056,13 @@
 def per_device_square(eigvecs, reflectors, factors, frequencies, region_blocks):
     local_blocks = eigvecs.shape[0] // BLOCK
     in_hbm = functools.partial(pltpu.with_memory_space_constraint, memory_space=pltpu.HBM)
-    x, y, w, g = prep(
-        region_blocks,
+    acc, sa, last = spread(
+        in_hbm(region_blocks),
         in_hbm(eigvecs.reshape(local_blocks, BLOCK, eigvecs.shape[1])),
         in_hbm(reflectors.reshape(2, local_blocks, BLOCK, reflectors.shape[2])),
+        factors,
+        frequencies.reshape(-1, 128),
     )
-    acc, sa, last = spread(x, y, w, g, factors, frequencies.reshape(-1, 128))
     return finish(acc, sa, last)
 
 

time: 125 us -> 117 us (0.936)
  the two profiles are of different devices: /device:TPU:6 before, /device:TPU:4 now
where the time goes in v2:
time: 117 us
  Pallas kernels  117 us (100%)
    pallas_call x1, Pallas kernels, spread(): pl.pallas_call(functools.partial(spread_kernel, chunks), out_shape=(pltpu...  113 us
    pallas_call x1, Pallas kernels, finish(): pl.pallas_call(finish_kernel, out_shape=jax.ShapeDtypeStruct(acc.shape, F...  4.09 us

profile of v2, /device:TPU:4, one launch (start us, length us, event | category | flops | bytes accessed | tf_op | source)
XLA Modules:
  0.0 116.7 jit_solution(10285057395585979670)
XLA Ops:
  0.0 112.6 %spread.1 = (f32[2304,1152]{1,0:T(8,128)S(1)}, bf16[8,2304,256]{2,1,0:T(8,128)(2,1)S(1)}, bf16[4,3,128,256]{3,2,1,0:T(8,128)(2,1)S(1)}) custom-call(s32[18]{0:T(128)} %index_ref.1, bf16[80,128,256]{2,1,0:T(8,128)(2,1)} %bitcast.3, bf16[2,80,128,128]{3,2,1,0:T(8,128)(2,1)} %bitcast.4, f32[2,128,128]{2,1,0:T(8,128)} %t_ref.1, f32[16,128]{1,0:T(8,128)} %bitcast.5), custom_call_target="tpu_custom_call" | custom-call | tf_op jit(solution)/shard_map/spread/pallas_call | solution.py:962
  112.6 4.1 %finish.1 = f32[2304,1152]{1,0:T(8,128)} custom-call(f32[2304,1152]{1,0:T(8,128)S(1)} %get-tuple-element.8.acc_ref, bf16[8,2304,256]{2,1,0:T(8,128)(2,1)S(1)} %get-tuple-element.9.sa_ref, bf16[4,3,128,256]{3,2,1,0:T(8,128)(2,1)S(1)} %get-tuple-element.10.last_ref), custom_call_target="tpu_custom_call" | custom-call | tf_op jit(solution)/shard_map/finish/pallas_call | solution.py:1045

commit v3 on v2

--- a/solution.py
+++ b/solution.py
@@ -395,7 +395,7 @@
 
 def spread_kernel(
     chunks, index_ref, vecs_ref, refl_ref, t_ref, f_ref, acc_ref, sa_ref, last_ref,
-    index, vecs, refl, w_sum, g_sum, w_ref, g_ref, index_sem, vec_sem, refl_sem, buf, tbuf, rbuf, w_in, g_in, g_full, p_full, weight,
+    index, vecs, refl, w_sum, g_sum, w_ref, index_sem, vec_sem, refl_sem, buf, tbuf, rbuf, w_in, g_in, g_full, p_full, weight,
     w_send, w_recv, g_send, g_recv, h_send, h_recv, p_send, p_recv,
     own_send, relay_send, zrel_send, zsrc_send, detz_send, deti_send, rr_send,
     ax, ay, ad, asib, zb, det, tz, rr,
@@ -423,17 +423,14 @@
 
     for d in range(1, 4):
         greet(lax.rem(r + d, 4), c)
-    for d in (1, 2):
-        for core in (0, 1):
-            greet(r, col(k ^ d, core))
-    greet(r, col(k, o))
+    for e in range(1, 8):
+        greet(r, c ^ e)
 
     def load(i):
         part = pl.ds(i * blocks, blocks)
         return (
             pltpu.make_async_copy(vecs_ref.at[part], vecs.at[part], vec_sem.at[i]),
-            pltpu.make_async_copy(refl_ref.at[0, part], refl.at[0, part], refl_sem.at[i, 0]),
-            pltpu.make_async_copy(refl_ref.at[1, part], refl.at[1, part], refl_sem.at[i, 1]),
+            pltpu.make_async_copy(refl_ref.at[:, part], refl.at[:, part], refl_sem.at[i]),
         )
 
     ahead = 3
@@ -461,10 +458,9 @@
         w_sum[...] = w
         g_sum[...] = g
     w_ref[...] = w.astype(BF)
-    g_ref[...] = g.astype(BF)
     index_copy.wait()
 
-    pl.semaphore_wait(barrier, 8)
+    pl.semaphore_wait(barrier, 10)
 
     def remote(src, dst, send, recv, row, column):
         return pltpu.make_async_remote_copy(
@@ -477,12 +473,12 @@
         part = pl.ds(pl.multiple_of(q * quarter, quarter), quarter)
         return remote(w_ref.at[part], w_in.at[d], w_send.at[d], w_recv.at[d], q, c)
 
-    g_half = width // 2
+    g_rows = width // 8
+    g_part = pl.ds(pl.multiple_of(c * g_rows, g_rows), g_rows)
 
     def g_copy(d):
         q = lax.rem(r + d, 4)
-        part = pl.ds(pl.multiple_of(h * g_half, g_half), g_half)
-        return remote(g_ref.at[part], g_in.at[d], g_send.at[d], g_recv.at[d], q, c)
+        return remote(g_sum.at[g_part], g_in.at[d], g_send.at[d], g_recv.at[d], q, c)
 
     for d in (2, 1, 3):
         g_copy(d).start()
@@ -497,15 +493,21 @@
     t0 = jnp.where(upper, t_ref[0], zero)
     t1 = jnp.where(upper, t_ref[1], zero)
 
-    g_part = pl.ds(pl.multiple_of(h * g_half, g_half), g_half)
     for d in (1, 2, 3):
         g_copy(d).wait_recv()
     value = g_sum[g_part, :]
     for d in (1, 2, 3):
-        value = value + g_in[d].astype(F32)
-    g_full[h] = value
-    h_copy = remote(g_full.at[h], g_full.at[h], h_send, h_recv, r, col(k, o))
-    h_copy.start()
+        value = value + g_in[d]
+    g_full[c] = value
+
+    def h_copy(e):
+        return remote(g_full.at[c], g_full.at[c], h_send.at[e], h_recv.at[e], r, c ^ e)
+
+    def h_arrival(e):
+        return remote(g_full.at[c ^ e], g_full.at[c ^ e], h_send.at[e], h_recv.at[e], r, c ^ e)
+
+    for e in range(1, 8):
+        h_copy(e).start()
     for d in (1, 2, 3):
         w_copy(d).wait_recv()
     mine = pl.ds(pl.multiple_of(r * quarter, quarter), quarter)
@@ -513,8 +515,9 @@
     for d in (1, 2, 3):
         w = w + w_in[d].astype(F32)
     second = dot_nt(w[:, width:], t1, precision=HIGH).astype(BF)
-    h_copy.wait_recv()
-    g = jnp.concatenate([g_full[0], g_full[1]], axis=0)
+    for e in range(1, 8):
+        h_arrival(e).wait_recv()
+    g = g_full[...].reshape(width, width)
     first = w[:, :width] - dot_nt(second.astype(F32), g, precision=HIGH)
     first = dot_nt(first, t0, precision=HIGH).astype(BF)
     p_full[r, :, :width] = first
@@ -548,7 +551,7 @@
     rank = jnp.where(is_low, r, 3 - r)
     away = jnp.where(is_low, -1, 1)
     slot = jnp.where(is_low, 0, 1)
-    early = 5
+    early = 3
 
     def det_own(hops, n):
         b = block_of(n)
@@ -711,24 +714,20 @@
 
         lax.fori_loop(0, half, one, 0)
 
-    tile = 256
+    tile = 2 * BLOCK
+    row_tile = acc_ref.shape[0] // 3
 
     def product(block, lane, size, third, places, add):
         at = mine_at + block
         lanes = pl.ds(pl.multiple_of(lane, BLOCK), size * BLOCK)
-
-        def one(i, _):
-            rows = pl.ds(pl.multiple_of(i * tile, tile), tile)
-            total = jnp.zeros((tile, size * BLOCK), F32)
-            for s in places:
-                right = buf[order[s], pl.ds(at, size)].reshape(size * BLOCK, columns)
-                total = total + dot_nt(sa_ref[s, rows, :], right)
-            if add:
-                total = total + acc_ref[rows, lanes]
-            acc_ref[rows, lanes] = total
-            return 0
-
-        lax.fori_loop(third * (n_tiles // 3), (third + 1) * (n_tiles // 3), one, 0)
+        rows = pl.ds(pl.multiple_of(third * row_tile, row_tile), row_tile)
+        total = jnp.zeros((row_tile, size * BLOCK), F32)
+        for s in places:
+            right = buf[order[s], pl.ds(at, size)].reshape(size * BLOCK, columns)
+            total = total + dot_nt(sa_ref[s, rows, :], right)
+        if add:
+            total = total + acc_ref[rows, lanes]
+        acc_ref[rows, lanes] = total
 
     def pair(q, third, places, add):
         product(2 * q, q * tile, 2, third, places, add)
@@ -761,7 +760,6 @@
 
     lax.fori_loop(0, half, first_third, 0)
 
-    n_tiles = acc_ref.shape[0] // tile
 
     def beat(u, _):
         def span(first, length):
@@ -797,9 +795,9 @@
 
         @pl.when(corner)
         def _():
-            n5 = (u - 5) // 2
-
-            @pl.when((rank == 1) & span(5, 2 * count) & (lax.rem(u, 2) == 1))
+            n5 = (u - 3) // 2
+
+            @pl.when((rank == 1) & span(3, 2 * count) & (lax.rem(u - 3, 2) == 0))
             def _():
                 for p in (3, 2):
                     det_z(p, n5).wait_recv()
@@ -810,18 +808,26 @@
                 det_own(1, u - 36 + early).start()
 
             v = u - 22
-            n22 = (2 * v) // 3
-
-            @pl.when(span(22, 27) & (lax.rem(v, 3) != 1))
-            def _():
-                for p in (3, 2):
-                    @pl.when(p > rank)
-                    def _():
-                        @pl.when(rank != 1)
-                        def _():
-                            det_z(p, n22).wait_recv()
-
-                        det_plane(p, n22).start()
+            n3 = (4 * v + 4) // 5
+
+            @pl.when((rank < 3) & span(22, 22) & (lax.rem(v, 5) != 4))
+            def _():
+                @pl.when(rank != 1)
+                def _():
+                    det_z(3, n3).wait_recv()
+
+                det_plane(3, n3).start()
+
+            v2 = u - 28
+            n2 = (2 * v2) // 3
+
+            @pl.when((rank < 2) & span(28, 27) & (lax.rem(v2, 3) != 1))
+            def _():
+                @pl.when(rank != 1)
+                def _():
+                    det_z(2, n2).wait_recv()
+
+                det_plane(2, n2).start()
 
             @pl.when((rank == 0) & (span(22, early) | span(40 + early, count - early)))
             def _():
@@ -902,7 +908,8 @@
         w_copy(d).wait_send()
         g_copy(d).wait_send()
         p_copy(d).wait_send()
-    h_copy.wait_send()
+    for e in range(1, 8):
+        h_copy(e).wait_send()
     shard = buf.at[0, pl.ds(0, count)]
     for way in (0, 1):
         drain(shard, own_send.at[way])
@@ -954,7 +961,7 @@
 def spread(index, vecs, refl, factors, frequencies):
     count = index.shape[0]
     columns, width = vecs.shape[2], refl.shape[3]
-    chunks = 10
+    chunks = 5
     half = count // 2
     dma = pltpu.SemaphoreType.DMA
     vmem = pl.BlockSpec(memory_space=pltpu.VMEM)
@@ -975,17 +982,16 @@
             pltpu.VMEM((columns, 2 * width), F32),
             pltpu.VMEM((width, width), F32),
             pltpu.VMEM((columns, 2 * width), BF),
-            pltpu.VMEM((width, width), BF),
-            dma, dma((chunks,)), dma((chunks, 2)),
+            dma, dma((chunks,)), dma((chunks,)),
             pltpu.VMEM((8, count + half, BLOCK, columns), BF),
             pltpu.VMEM((3, count, BLOCK, columns), BF),
             pltpu.VMEM((2, half, BLOCK, columns), BF),
             pltpu.VMEM((4, columns // 4, 2 * width), BF),
-            pltpu.VMEM((4, width // 2, width), BF),
-            pltpu.VMEM((2, width // 2, width), F32),
+            pltpu.VMEM((4, width // 8, width), F32),
+            pltpu.VMEM((8, width // 8, width), F32),
             pltpu.VMEM((4, columns // 4, 2 * width), BF),
             pltpu.VMEM(frequencies.shape, F32),
-            dma((4,)), dma((4,)), dma((4,)), dma((4,)), dma, dma, dma((4,)), dma((4,)),
+            dma((4,)), dma((4,)), dma((4,)), dma((4,)), dma((8,)), dma((8,)), dma((4,)), dma((4,)),
             dma((3,)), dma((2,)), dma, dma((2,)), dma((4,)), dma((4,)), dma((2,)),
             dma((count,)), dma((count,)), dma((count,)), dma((4, count)),
             dma((3 * count,)), dma((2, half)), dma((3, count)), dma((2, half)),

time: 117 us -> 113 us (0.966)
  the two profiles are of different devices: /device:TPU:4 before, /device:TPU:6 now
where the time goes in v3:
time: 113 us
  Pallas kernels  113 us (100%)
    pallas_call x1, Pallas kernels, spread(): pl.pallas_call(functools.partial(spread_kernel, chunks), out_shape=(pltpu...  109 us
    pallas_call x1, Pallas kernels, finish(): pl.pallas_call(finish_kernel, out_shape=jax.ShapeDtypeStruct(acc.shape, F...  4.09 us

profile of v3, /device:TPU:6, one launch (start us, length us, event | category | flops | bytes accessed | tf_op | source)
XLA Modules:
  0.0 113.1 jit_solution(11239960479115736704)
XLA Ops:
  0.0 109.0 %spread.1 = (f32[2304,1152]{1,0:T(8,128)S(1)}, bf16[8,2304,256]{2,1,0:T(8,128)(2,1)S(1)}, bf16[4,3,128,256]{3,2,1,0:T(8,128)(2,1)S(1)}) custom-call(s32[18]{0:T(128)} %index_ref.1, bf16[80,128,256]{2,1,0:T(8,128)(2,1)} %bitcast.3, bf16[2,80,128,128]{3,2,1,0:T(8,128)(2,1)} %bitcast.4, f32[2,128,128]{2,1,0:T(8,128)} %t_ref.1, f32[16,128]{1,0:T(8,128)} %bitcast.5), custom_call_target="tpu_custom_call" | custom-call | tf_op jit(solution)/shard_map/spread/pallas_call | solution.py:969
  109.0 4.1 %finish.1 = f32[2304,1152]{1,0:T(8,128)} custom-call(f32[2304,1152]{1,0:T(8,128)S(1)} %get-tuple-element.8.acc_ref, bf16[8,2304,256]{2,1,0:T(8,128)(2,1)S(1)} %get-tuple-element.9.sa_ref, bf16[4,3,128,256]{3,2,1,0:T(8,128)(2,1)S(1)} %get-tuple-element.10.last_ref), custom_call_target="tpu_custom_call" | custom-call | tf_op jit(solution)/shard_map/finish/pallas_call | solution.py:1051

commit v4 on v3

--- a/solution.py
+++ b/solution.py
@@ -394,8 +394,8 @@
 
 
 def spread_kernel(
-    chunks, index_ref, vecs_ref, refl_ref, t_ref, f_ref, acc_ref, sa_ref, last_ref,
-    index, vecs, refl, w_sum, g_sum, w_ref, index_sem, vec_sem, refl_sem, buf, tbuf, rbuf, w_in, g_in, g_full, p_full, weight,
+    chunks, index_ref, vecs_ref, refl_ref, factor_ref, freq_ref, acc_ref, sa_ref, last_ref,
+    index, vecs, refl, w_sum, g_sum, w_ref, t_ref, f_ref, small_sem, vec_sem, refl_sem, buf, tbuf, rbuf, w_in, g_in, g_full, p_full, weight,
     w_send, w_recv, g_send, g_recv, h_send, h_recv, p_send, p_recv,
     own_send, relay_send, zrel_send, zsrc_send, detz_send, deti_send, rr_send,
     ax, ay, ad, asib, zb, det, tz, rr,
@@ -426,39 +426,36 @@
     for e in range(1, 8):
         greet(r, c ^ e)
 
-    def load(i):
+    def load_vecs(i):
         part = pl.ds(i * blocks, blocks)
-        return (
-            pltpu.make_async_copy(vecs_ref.at[part], vecs.at[part], vec_sem.at[i]),
-            pltpu.make_async_copy(refl_ref.at[:, part], refl.at[:, part], refl_sem.at[i]),
-        )
-
-    ahead = 3
-    for i in range(ahead):
-        for copy in load(i):
-            copy.start()
-    index_copy = pltpu.make_async_copy(index_ref, index, index_sem)
-    index_copy.start()
-    rows = blocks * BLOCK
+        return pltpu.make_async_copy(vecs_ref.at[part], vecs.at[part], vec_sem.at[i])
+
+    def load_refl(i):
+        part = pl.ds(i * blocks, blocks)
+        return pltpu.make_async_copy(refl_ref.at[:, part], refl.at[:, part], refl_sem.at[i])
+
+    def rows_of(array, i):
+        return array[pl.ds(i * blocks, blocks)].reshape(blocks * BLOCK, array.shape[2])
+
     for i in range(chunks):
-        if i + ahead < chunks:
-            for copy in load(i + ahead):
-                copy.start()
-        for copy in load(i):
-            copy.wait()
-        part = pl.ds(i * blocks, blocks)
-        e = vecs[part].reshape(rows, columns)
-        y0 = refl[0, part].reshape(rows, width)
-        y1 = refl[1, part].reshape(rows, width)
-        w = dot_tn(e, jnp.concatenate([y0, y1], axis=1))
-        g = dot_tn(y0, y1)
+        load_refl(i).start()
+    load_vecs(0).start()
+    small = [
+        pltpu.make_async_copy(src, dst, small_sem.at[i])
+        for i, (src, dst) in enumerate(((index_ref, index), (factor_ref, t_ref), (freq_ref, f_ref)))
+    ]
+    for copy in small:
+        copy.start()
+    for i in range(chunks):
+        if i + 1 < chunks:
+            load_vecs(i + 1).start()
+        load_refl(i).wait()
+        g = dot_tn(rows_of(refl.at[0], i), rows_of(refl.at[1], i))
         if i:
-            w = w + w_sum[...]
             g = g + g_sum[...]
-        w_sum[...] = w
         g_sum[...] = g
-    w_ref[...] = w.astype(BF)
-    index_copy.wait()
+    for copy in small:
+        copy.wait()
 
     pl.semaphore_wait(barrier, 10)
 
@@ -468,21 +465,51 @@
             device_id=(row, column), device_id_type=MESH,
         )
 
-    def w_copy(d):
-        q = lax.rem(r + d, 4)
-        part = pl.ds(pl.multiple_of(q * quarter, quarter), quarter)
-        return remote(w_ref.at[part], w_in.at[d], w_send.at[d], w_recv.at[d], q, c)
+    far = [jnp.where(r < 2, 3, 0), jnp.where(r < 2, 2, 1), jnp.where(r < 2, 1 - r, 5 - r)]
+
+    def w_copy(q, part):
+        d = lax.rem(q - r + 4, 4)
+        rows = pl.ds(pl.multiple_of(q * quarter, quarter), quarter)
+        lanes = pl.ds(part * width, width)
+        return remote(
+            w_ref.at[rows, lanes], w_in.at[d, :, lanes], w_send.at[d, part], w_recv.at[d, part], q, c
+        )
 
     g_rows = width // 8
     g_part = pl.ds(pl.multiple_of(c * g_rows, g_rows), g_rows)
 
-    def g_copy(d):
-        q = lax.rem(r + d, 4)
+    def g_copy(q):
+        d = lax.rem(q - r + 4, 4)
         return remote(g_sum.at[g_part], g_in.at[d], g_send.at[d], g_recv.at[d], q, c)
 
-    for d in (2, 1, 3):
-        g_copy(d).start()
-        w_copy(d).start()
+    for q in far:
+        g_copy(q).start()
+    for i in range(chunks):
+        load_vecs(i).wait()
+        y = jnp.concatenate([rows_of(refl.at[0], i), rows_of(refl.at[1], i)], axis=1)
+        w = dot_tn(rows_of(vecs, i), y)
+        if i:
+            w = w + w_sum[...]
+        w_sum[...] = w
+    w_ref[...] = w.astype(BF)
+    for part in (1, 0):
+        for q in far:
+            w_copy(q, part).start()
+    for q in far:
+        g_copy(q).wait_recv()
+    value = g_sum[g_part, :]
+    for d in (1, 2, 3):
+        value = value + g_in[d]
+    g_full[c] = value
+
+    def h_copy(e):
+        return remote(g_full.at[c], g_full.at[c], h_send.at[e], h_recv.at[e], r, c ^ e)
+
+    def h_arrival(e):
+        return remote(g_full.at[c ^ e], g_full.at[c ^ e], h_send.at[e], h_recv.at[e], r, c ^ e)
+
+    for e in range(1, 8):
+        h_copy(e).start()
 
     f = f_ref[...]
     weight[...] = 1.0 / jnp.tanh(f / 2.0) / (2.0 * f)
@@ -493,47 +520,42 @@
     t0 = jnp.where(upper, t_ref[0], zero)
     t1 = jnp.where(upper, t_ref[1], zero)
 
-    for d in (1, 2, 3):
-        g_copy(d).wait_recv()
-    value = g_sum[g_part, :]
-    for d in (1, 2, 3):
-        value = value + g_in[d]
-    g_full[c] = value
-
-    def h_copy(e):
-        return remote(g_full.at[c], g_full.at[c], h_send.at[e], h_recv.at[e], r, c ^ e)
-
-    def h_arrival(e):
-        return remote(g_full.at[c ^ e], g_full.at[c ^ e], h_send.at[e], h_recv.at[e], r, c ^ e)
-
-    for e in range(1, 8):
-        h_copy(e).start()
-    for d in (1, 2, 3):
-        w_copy(d).wait_recv()
     mine = pl.ds(pl.multiple_of(r * quarter, quarter), quarter)
-    w = w_sum[mine, :]
-    for d in (1, 2, 3):
-        w = w + w_in[d].astype(F32)
-    second = dot_nt(w[:, width:], t1, precision=HIGH).astype(BF)
+
+    def w_total(part):
+        lanes = pl.ds(part * width, width)
+        for q in far:
+            w_copy(q, part).wait_recv()
+        w = w_sum[mine, lanes]
+        for d in (1, 2, 3):
+            w = w + w_in[d, :, lanes].astype(F32)
+        return w
+
+    def p_copy(q, part):
+        d = lax.rem(q - r + 4, 4)
+        at = p_full.at[r, :, pl.ds(part * width, width)]
+        return remote(at, at, p_send.at[d, part], p_recv.at[d, part], q, c)
+
+    def p_arrival(q, part):
+        d = lax.rem(r - q + 4, 4)
+        at = p_full.at[q, :, pl.ds(part * width, width)]
+        return remote(at, at, p_send.at[d, part], p_recv.at[d, part], q, c)
+
+    second = dot_nt(w_total(1), t1, precision=HIGH).astype(BF)
+    p_full[r, :, width:] = second
+    for q in far:
+        p_copy(q, 1).start()
+    first = w_total(0)
     for e in range(1, 8):
         h_arrival(e).wait_recv()
     g = g_full[...].reshape(width, width)
-    first = w[:, :width] - dot_nt(second.astype(F32), g, precision=HIGH)
-    first = dot_nt(first, t0, precision=HIGH).astype(BF)
-    p_full[r, :, :width] = first
-    p_full[r, :, width:] = second
-
-    def p_copy(d):
-        return remote(p_full.at[r], p_full.at[r], p_send.at[d], p_recv.at[d], lax.rem(r + d, 4), c)
-
-    def p_arrival(d):
-        q = lax.rem(r + d, 4)
-        return remote(p_full.at[q], p_full.at[q], p_send.at[d], p_recv.at[4 - d], q, c)
-
-    for d in (2, 1, 3):
-        p_copy(d).start()
-    for d in (1, 2, 3):
-        p_arrival(d).wait_recv()
+    first = first - dot_nt(second.astype(F32), g, precision=HIGH)
+    p_full[r, :, :width] = dot_nt(first, t0, precision=HIGH).astype(BF)
+    for q in far:
+        p_copy(q, 0).start()
+    for part in (1, 0):
+        for q in far:
+            p_arrival(q, part).wait_recv()
 
     def block_of(n):
         return lax.rem(n, 2) * half + n // 2
@@ -551,7 +573,7 @@
     rank = jnp.where(is_low, r, 3 - r)
     away = jnp.where(is_low, -1, 1)
     slot = jnp.where(is_low, 0, 1)
-    early = 3
+    early = 4
 
     def det_own(hops, n):
         b = block_of(n)
@@ -829,9 +851,9 @@
 
                 det_plane(2, n2).start()
 
-            @pl.when((rank == 0) & (span(22, early) | span(40 + early, count - early)))
-            def _():
-                n = jnp.where(u < 40, u - 22, u - 40)
+            @pl.when((rank == 0) & (span(22, early) | span(39 + early, count - early)))
+            def _():
+                n = jnp.where(u < 40, u - 22, u - 39)
                 det_z(1, n).wait_recv()
                 det_plane(1, n).start()
 
@@ -904,10 +926,11 @@
     def drain(ref, sem):
         pltpu.make_async_copy(ref, ref, sem).wait()
 
-    for d in (1, 2, 3):
-        w_copy(d).wait_send()
-        g_copy(d).wait_send()
-        p_copy(d).wait_send()
+    for q in far:
+        g_copy(q).wait_send()
+        for part in (0, 1):
+            w_copy(q, part).wait_send()
+            p_copy(q, part).wait_send()
     for e in range(1, 8):
         h_copy(e).wait_send()
     shard = buf.at[0, pl.ds(0, count)]
@@ -973,7 +996,7 @@
             pltpu.VMEM((8, count * BLOCK, columns), BF),
             pltpu.VMEM((4, 3, BLOCK, columns), BF),
         ),
-        in_specs=[hbm] * 3 + [vmem] * 2,
+        in_specs=[hbm] * 5,
         out_specs=(vmem,) * 3,
         scratch_shapes=[
             pltpu.SMEM((count,), jnp.int32),
@@ -982,7 +1005,9 @@
             pltpu.VMEM((columns, 2 * width), F32),
             pltpu.VMEM((width, width), F32),
             pltpu.VMEM((columns, 2 * width), BF),
-            dma, dma((chunks,)), dma((chunks,)),
+            pltpu.VMEM(factors.shape, F32),
+            pltpu.VMEM(frequencies.shape, F32),
+            dma((3,)), dma((chunks,)), dma((chunks,)),
             pltpu.VMEM((8, count + half, BLOCK, columns), BF),
             pltpu.VMEM((3, count, BLOCK, columns), BF),
             pltpu.VMEM((2, half, BLOCK, columns), BF),
@@ -991,7 +1016,7 @@
             pltpu.VMEM((8, width // 8, width), F32),
             pltpu.VMEM((4, columns // 4, 2 * width), BF),
             pltpu.VMEM(frequencies.shape, F32),
-            dma((4,)), dma((4,)), dma((4,)), dma((4,)), dma((8,)), dma((8,)), dma((4,)), dma((4,)),
+            dma((4, 2)), dma((4, 2)), dma((4,)), dma((4,)), dma((8,)), dma((8,)), dma((4, 2)), dma((4, 2)),
             dma((3,)), dma((2,)), dma, dma((2,)), dma((4,)), dma((4,)), dma((2,)),
             dma((count,)), dma((count,)), dma((count,)), dma((4, count)),
             dma((3 * count,)), dma((2, half)), dma((3, count)), dma((2, half)),
@@ -1066,8 +1091,8 @@
         in_hbm(region_blocks),
         in_hbm(eigvecs.reshape(local_blocks, BLOCK, eigvecs.shape[1])),
         in_hbm(reflectors.reshape(2, local_blocks, BLOCK, reflectors.shape[2])),
-        factors,
-        frequencies.reshape(-1, 128),
+        in_hbm(factors),
+        in_hbm(frequencies.reshape(-1, 128)),
     )
     return finish(acc, sa, last)
 

time: 113 us -> 111 us (0.982)
  Pallas kernels: 113 us -> 110 us
    pallas_call x1, Pallas kernels: 109 us -> 106 us  [spread(): pl.pallas_call(functools.partial(spread_kernel, chunks), out_shape=(pltpu...]
where the time goes in v4:
time: 111 us; the launch traced here: 110 us
  Pallas kernels  110 us (99%)
    pallas_call x1, Pallas kernels, spread(): pl.pallas_call(functools.partial(spread_kernel, chunks), out_shape=(pltpu...  106 us
    pallas_call x1, Pallas kernels, finish(): pl.pallas_call(finish_kernel, out_shape=jax.ShapeDtypeStruct(acc.shape, F...  4.09 us

profile of v4, /device:TPU:6, one launch (start us, length us, event | category | flops | bytes accessed | tf_op | source)
XLA Modules:
  0.0 110.5 jit_solution(11105607994367755011)
XLA Ops:
  0.0 106.4 %spread.1 = (f32[2304,1152]{1,0:T(8,128)S(1)}, bf16[8,2304,256]{2,1,0:T(8,128)(2,1)S(1)}, bf16[4,3,128,256]{3,2,1,0:T(8,128)(2,1)S(1)}) custom-call(s32[18]{0:T(128)} %index_ref.1, bf16[80,128,256]{2,1,0:T(8,128)(2,1)} %bitcast.3, bf16[2,80,128,128]{3,2,1,0:T(8,128)(2,1)} %bitcast.4, f32[2,128,128]{2,1,0:T(8,128)} %factor_ref.1, f32[16,128]{1,0:T(8,128)} %bitcast.5), custom_call_target="tpu_custom_call" | custom-call | tf_op jit(solution)/shard_map/spread/pallas_call | solution.py:992
  106.4 4.1 %finish.1 = f32[2304,1152]{1,0:T(8,128)} custom-call(f32[2304,1152]{1,0:T(8,128)S(1)} %get-tuple-element.8.acc_ref, bf16[8,2304,256]{2,1,0:T(8,128)(2,1)S(1)} %get-tuple-element.9.sa_ref, bf16[4,3,128,256]{3,2,1,0:T(8,128)(2,1)S(1)} %get-tuple-element.10.last_ref), custom_call_target="tpu_custom_call" | custom-call | tf_op jit(solution)/shard_map/finish/pallas_call | solution.py:1076

commit v5 on v4

--- a/solution.py
+++ b/solution.py
@@ -575,6 +575,19 @@
     slot = jnp.where(is_low, 0, 1)
     early = 4
 
+    extra = 2
+    near = count - extra
+
+    def det_more(hops, i):
+        b = half - 1 + i * half
+        return remote(
+            buf.at[col(k ^ 1, h), b], tbuf.at[rank - 1, count + i], detz_send.at[hops - 1],
+            tz.at[rank - 1, count + i], r + away * hops, c,
+        )
+
+    def slot_of(n):
+        return jnp.where(n < count, block_of(n), n)
+
     def det_own(hops, n):
         b = block_of(n)
         return remote(
@@ -614,11 +627,11 @@
     def z_source_step(t):
         @pl.when(at_source)
         def _():
-            @pl.when(r > 0)
+            @pl.when((r > 0) & ((k < 3) | (t < steps - extra)))
             def _():
                 z_source(t, True).start()
 
-            @pl.when(r < last_row)
+            @pl.when((r < last_row) & ((k > 0) | (t < steps - extra)))
             def _():
                 z_source(t, False).start()
 
@@ -676,12 +689,11 @@
         return remote(at, at, relay_send.at[way], ad.at[n], r, col(to, h))
 
     def det_z(p, n):
-        at = tbuf.at[p - 1, block_of(n)]
+        at = tbuf.at[p - 1, slot_of(n)]
         return remote(at, at, detz_send.at[p], tz.at[p - 1, n], r + away, c)
 
     def det_plane(p, n):
-        b = block_of(n)
-        src = tbuf.at[p - 1, b]
+        src = tbuf.at[p - 1, slot_of(n)]
         core = lax.rem(n, 2)
         if p < 3:
             return remote(
@@ -697,15 +709,16 @@
 
     def rr_copy(way, n):
         low = k - 1 if way == 0 else 2 - k
-        src = low if way == 0 else low + 6
+        more = (n == half).astype(jnp.int32)
+        src = low + 2 * more if way == 0 else low + 6 - 2 * more
         return remote(
-            rbuf.at[way, n], buf.at[src, count + n], rr_send.at[way], det.at[low, n],
+            rbuf.at[way, n], buf.at[src, count + n - more], rr_send.at[way], det.at[low, n],
             r, col(3 if way == 0 else 0, h),
         )
 
-    def det_arrival(low, n):
-        src = jnp.where(down, low, low + 6)
-        at = buf.at[src, count + n]
+    def det_arrival(low, n, more=0):
+        src = jnp.where(down, low + 2 * more, low + 6 - 2 * more)
+        at = buf.at[src, count + n - more]
         return remote(at, at, own_send.at[2], det.at[low, n], r, col(k, o))
 
     mine_at = jnp.where(at_source, h * half, count)
@@ -754,6 +767,20 @@
     def pair(q, third, places, add):
         product(2 * q, q * tile, 2, third, places, add)
 
+    def straight(e):
+        core = lax.rem(h + e, 2)
+        src = col(k ^ 1, core)
+        return remote(
+            buf.at[src, h * half + half - 1], buf.at[src, count + half - 1], detz_send.at[e],
+            det.at[core, half - 1], r + jnp.where(k == 1, -1, 1), c,
+        )
+
+    def wait_more():
+        @pl.when(jnp.logical_not(at_source) & (depth == 3))
+        def _():
+            for low in (0, 1):
+                det_arrival(low, half, 1).wait_recv()
+
     def wait_detours(n):
         @pl.when(jnp.logical_not(at_source))
         def _():
@@ -766,7 +793,7 @@
     def z_relay_step(u):
         t = u - lag * hops
 
-        @pl.when(jnp.logical_not(at_source) & (t >= 0) & (t < steps))
+        @pl.when(jnp.logical_not(at_source) & (t >= 0) & (t < jnp.where(depth == 3, steps - extra, steps)))
         def _():
             z_relay(t).wait_recv()
 
@@ -819,20 +846,29 @@
         def _():
             n5 = (u - 3) // 2
 
-            @pl.when((rank == 1) & span(3, 2 * count) & (lax.rem(u - 3, 2) == 0))
-            def _():
-                for p in (3, 2):
-                    det_z(p, n5).wait_recv()
-                    det_z(p, n5).start()
-
-            @pl.when((rank == 1) & span(36, count - early))
+            @pl.when((rank == 1) & span(3, 2 * (count + extra)) & (lax.rem(u - 3, 2) == 0))
+            def _():
+                det_z(3, n5).wait_recv()
+                det_z(3, n5).start()
+
+                @pl.when(n5 < count)
+                def _():
+                    det_z(2, n5).wait_recv()
+                    det_z(2, n5).start()
+
+            @pl.when((rank == 3) & span(20, extra))
+            def _():
+                det_more(2, u - 20).start()
+                det_more(1, u - 20).start()
+
+            @pl.when((rank == 1) & span(36, near - early))
             def _():
                 det_own(1, u - 36 + early).start()
 
             v = u - 22
             n3 = (4 * v + 4) // 5
 
-            @pl.when((rank < 3) & span(22, 22) & (lax.rem(v, 5) != 4))
+            @pl.when((rank < 3) & span(22, 24) & (lax.rem(v, 5) != 4))
             def _():
                 @pl.when(rank != 1)
                 def _():
@@ -851,16 +887,18 @@
 
                 det_plane(2, n2).start()
 
-            @pl.when((rank == 0) & (span(22, early) | span(39 + early, count - early)))
+            @pl.when((rank == 0) & (span(22, early) | span(39 + early, near - early)))
             def _():
                 n = jnp.where(u < 40, u - 22, u - 39)
                 det_z(1, n).wait_recv()
                 det_plane(1, n).start()
 
-        w = u - 26 - 2 * h
-        @pl.when(between & (w >= 0) & (w < 3 * half) & (lax.rem(w, 3) == 0))
-        def _():
-            n = w // 3
+        w = u - 30
+        item = (4 * w + 4) // 5
+
+        @pl.when(between & span(30, 24) & (lax.rem(w, 5) != 4) & (lax.rem(item, 2) == h))
+        def _():
+            n = item // 2
             for way in (0, 1):
                 @pl.when(r < last_row if way == 0 else r > 0)
                 def _():
@@ -884,6 +922,11 @@
         def _():
             z_source_step(u + 2 * count - 27)
 
+        @pl.when(at_source & (u == 36) & ((k == 1) | (k == 2)))
+        def _():
+            for e in (0, 1):
+                straight(e).start()
+
         for first, length, place in ((6, 4, 0), (22, 4, 2), (34, 8, 4)):
             @pl.when(span(first, length))
             def _():
@@ -910,16 +953,17 @@
         def _():
             pair(q, i, range(4, 8), True)
 
-        @pl.when(span(57, 3))
-        def _():
-            product(8, 4 * tile, 1, u - 57, range(4), False)
+        @pl.when((u == 47) | (u == 51) | (u == 55))
+        def _():
+            product(8, 4 * tile, 1, (u - 47) // 4, range(4), False)
 
         return 0
 
-    lax.fori_loop(0, steps + 3 * lag, beat, 0)
+    lax.fori_loop(0, steps + 2 * lag, beat, 0)
     wait_detours(6)
     wait_detours(7)
     wait_detours(8)
+    wait_more()
     for s in range(4):
         last_ref[s] = buf[order[4 + s], pl.ds(mine_at + 6, 3)]
 
@@ -939,39 +983,61 @@
         drain(buf.at[0, pl.ds(0, half)], relay_send.at[way])
     drain(buf.at[:, pl.ds(0, half)], own_send.at[2])
 
+    whole = buf.at[pl.ds(0, 2)]
+    short = buf.at[pl.ds(0, 2), pl.ds(0, count + half - extra // 2)]
+    longer = buf.at[0, pl.ds(0, count + extra)]
+    brief = buf.at[0, pl.ds(0, near)]
+
+    @pl.when(at_source & ((k == 1) | (k == 2)))
+    def _():
+        for e in (0, 1):
+            straight(e).wait_send()
+
+    def drain_either(is_short, sem):
+        @pl.when(is_short)
+        def _():
+            drain(short, sem)
+
+        @pl.when(jnp.logical_not(is_short))
+        def _():
+            drain(whole, sem)
+
     @pl.when(at_source)
     def _():
         @pl.when(r > 0)
         def _():
-            drain(buf.at[pl.ds(0, 2)], zsrc_send.at[0])
+            drain_either(k == 3, zsrc_send.at[0])
 
         @pl.when(r < last_row)
         def _():
-            drain(buf.at[pl.ds(0, 2)], zsrc_send.at[1])
+            drain_either(k == 0, zsrc_send.at[1])
 
     @pl.when((down & (r > 0)) | ((r > k) & (r < last_row)))
     def _():
-        drain(buf.at[pl.ds(0, 2)], zrel_send)
+        drain_either(depth == 3, zrel_send)
 
     @pl.when(corner)
     def _():
         for p in (3, 2, 1):
             @pl.when(p > rank)
             def _():
-                drain(shard, deti_send.at[p])
+                drain({1: brief, 2: shard, 3: longer}[p], deti_send.at[p])
 
         @pl.when(rank == 1)
         def _():
-            for p in (3, 2):
-                drain(shard, detz_send.at[p])
-
-        @pl.when(rank > 0)
+            drain(longer, detz_send.at[3])
+            drain(shard, detz_send.at[2])
+
+            drain(brief, detz_send.at[0])
+
+        @pl.when(rank == 2)
         def _():
             drain(shard, detz_send.at[0])
 
         @pl.when(rank == 3)
         def _():
-            drain(shard, detz_send.at[1])
+            drain(longer, detz_send.at[0])
+            drain(longer, detz_send.at[1])
 
     @pl.when(between)
     def _():
@@ -1009,8 +1075,8 @@
             pltpu.VMEM(frequencies.shape, F32),
             dma((3,)), dma((chunks,)), dma((chunks,)),
             pltpu.VMEM((8, count + half, BLOCK, columns), BF),
-            pltpu.VMEM((3, count, BLOCK, columns), BF),
-            pltpu.VMEM((2, half, BLOCK, columns), BF),
+            pltpu.VMEM((3, count + 2, BLOCK, columns), BF),
+            pltpu.VMEM((2, half + 1, BLOCK, columns), BF),
             pltpu.VMEM((4, columns // 4, 2 * width), BF),
             pltpu.VMEM((4, width // 8, width), F32),
             pltpu.VMEM((8, width // 8, width), F32),
@@ -1019,7 +1085,7 @@
             dma((4, 2)), dma((4, 2)), dma((4,)), dma((4,)), dma((8,)), dma((8,)), dma((4, 2)), dma((4, 2)),
             dma((3,)), dma((2,)), dma, dma((2,)), dma((4,)), dma((4,)), dma((2,)),
             dma((count,)), dma((count,)), dma((count,)), dma((4, count)),
-            dma((3 * count,)), dma((2, half)), dma((3, count)), dma((2, half)),
+            dma((3 * count,)), dma((2, half + 1)), dma((3, count + 2)), dma((2, half + 1)),
         ],
         compiler_params=pltpu.CompilerParams(
             collective_id=2, has_side_effects=True, vmem_limit_bytes=36 << 20

time: 111 us -> 108 us (0.973)
  Pallas kernels: 110 us -> 108 us
    pallas_call x1, Pallas kernels: 106 us -> 104 us  [spread(): pl.pallas_call(functools.partial(spread_kernel, chunks), out_shape=(pltpu...]
where the time goes in v5:
time: 108 us
  Pallas kernels  108 us (100%)
    pallas_call x1, Pallas kernels, spread(): pl.pallas_call(functools.partial(spread_kernel, chunks), out_shape=(pltpu...  104 us
    pallas_call x1, Pallas kernels, finish(): pl.pallas_call(finish_kernel, out_shape=jax.ShapeDtypeStruct(acc.shape, F...  4.09 us

profile of v5, /device:TPU:6, one launch (start us, length us, event | category | flops | bytes accessed | tf_op | source)
XLA Modules:
  0.0 107.8 jit_solution(18390798940589956496)
XLA Ops:
  0.0 103.7 %spread.1 = (f32[2304,1152]{1,0:T(8,128)S(1)}, bf16[8,2304,256]{2,1,0:T(8,128)(2,1)S(1)}, bf16[4,3,128,256]{3,2,1,0:T(8,128)(2,1)S(1)}) custom-call(s32[18]{0:T(128)} %index_ref.1, bf16[80,128,256]{2,1,0:T(8,128)(2,1)} %bitcast.3, bf16[2,80,128,128]{3,2,1,0:T(8,128)(2,1)} %bitcast.4, f32[2,128,128]{2,1,0:T(8,128)} %factor_ref.1, f32[16,128]{1,0:T(8,128)} %bitcast.5), custom_call_target="tpu_custom_call" | custom-call | tf_op jit(solution)/shard_map/spread/pallas_call | solution.py:1058
  103.7 4.1 %finish.1 = f32[2304,1152]{1,0:T(8,128)} custom-call(f32[2304,1152]{1,0:T(8,128)S(1)} %get-tuple-element.8.acc_ref, bf16[8,2304,256]{2,1,0:T(8,128)(2,1)S(1)} %get-tuple-element.9.sa_ref, bf16[4,3,128,256]{3,2,1,0:T(8,128)(2,1)S(1)} %get-tuple-element.10.last_ref), custom_call_target="tpu_custom_call" | custom-call | tf_op jit(solution)/shard_map/finish/pallas_call | solution.py:1142

commit v6 on v5

--- a/solution.py
+++ b/solution.py
@@ -814,7 +814,6 @@
         def span(first, length):
             return (u >= first) & (u < first + length)
 
-        z_relay_step(u)
 
         @pl.when(span(2, count))
         def _():
@@ -921,6 +920,8 @@
         @pl.when(span(27, count))
         def _():
             z_source_step(u + 2 * count - 27)
+
+        z_relay_step(u)
 
         @pl.when(at_source & (u == 36) & ((k == 1) | (k == 2)))
         def _():

time: 108 us -> 108 us (level)
  no operation moved by 1% of the time
where the time goes in v6:
time: 108 us
  Pallas kernels  108 us (100%)
    pallas_call x1, Pallas kernels, spread(): pl.pallas_call(functools.partial(spread_kernel, chunks), out_shape=(pltpu...  104 us
    pallas_call x1, Pallas kernels, finish(): pl.pallas_call(finish_kernel, out_shape=jax.ShapeDtypeStruct(acc.shape, F...  4.09 us

profile of v6, /device:TPU:6, one launch (start us, length us, event | category | flops | bytes accessed | tf_op | source)
XLA Modules:
  0.0 107.7 jit_solution(9804313926324358347)
XLA Ops:
  0.0 103.6 %spread.1 = (f32[2304,1152]{1,0:T(8,128)S(1)}, bf16[8,2304,256]{2,1,0:T(8,128)(2,1)S(1)}, bf16[4,3,128,256]{3,2,1,0:T(8,128)(2,1)S(1)}) custom-call(s32[18]{0:T(128)} %index_ref.1, bf16[80,128,256]{2,1,0:T(8,128)(2,1)} %bitcast.3, bf16[2,80,128,128]{3,2,1,0:T(8,128)(2,1)} %bitcast.4, f32[2,128,128]{2,1,0:T(8,128)} %factor_ref.1, f32[16,128]{1,0:T(8,128)} %bitcast.5), custom_call_target="tpu_custom_call" | custom-call | tf_op jit(solution)/shard_map/spread/pallas_call | solution.py:1059
  103.6 4.1 %finish.1 = f32[2304,1152]{1,0:T(8,128)} custom-call(f32[2304,1152]{1,0:T(8,128)S(1)} %get-tuple-element.8.acc_ref, bf16[8,2304,256]{2,1,0:T(8,128)(2,1)S(1)} %get-tuple-element.9.sa_ref, bf16[4,3,128,256]{3,2,1,0:T(8,128)(2,1)S(1)} %get-tuple-element.10.last_ref), custom_call_target="tpu_custom_call" | custom-call | tf_op jit(solution)/shard_map/finish/pallas_call | solution.py:1143

commit v7 on v6

--- a/solution.py
+++ b/solution.py
@@ -1098,7 +1098,7 @@
 def finish_kernel(acc_ref, sa_ref, last_ref, out_ref, tail, sem, pair_sem, single_sem):
     rows, columns = acc_ref.shape
     held, blocks, lane, depth = last_ref.shape
-    parts = 4
+    parts = 2
     size = rows // parts
     done = columns - blocks * lane
 

time: 108 us -> 108 us (level)
  no operation moved by 1% of the time
where the time goes in v7:
time: 108 us
  Pallas kernels  108 us (100%)
    pallas_call x1, Pallas kernels, spread(): pl.pallas_call(functools.partial(spread_kernel, chunks), out_shape=(pltpu...  104 us
    pallas_call x1, Pallas kernels, finish(): pl.pallas_call(finish_kernel, out_shape=jax.ShapeDtypeStruct(acc.shape, F...  4.15 us

profile of v7, /device:TPU:6, one launch (start us, length us, event | category | flops | bytes accessed | tf_op | source)
XLA Modules:
  0.0 107.7 jit_solution(6210342226182389302)
XLA Ops:
  0.0 103.6 %spread.1 = (f32[2304,1152]{1,0:T(8,128)S(1)}, bf16[8,2304,256]{2,1,0:T(8,128)(2,1)S(1)}, bf16[4,3,128,256]{3,2,1,0:T(8,128)(2,1)S(1)}) custom-call(s32[18]{0:T(128)} %index_ref.1, bf16[80,128,256]{2,1,0:T(8,128)(2,1)} %bitcast.3, bf16[2,80,128,128]{3,2,1,0:T(8,128)(2,1)} %bitcast.4, f32[2,128,128]{2,1,0:T(8,128)} %factor_ref.1, f32[16,128]{1,0:T(8,128)} %bitcast.5), custom_call_target="tpu_custom_call" | custom-call | tf_op jit(solution)/shard_map/spread/pallas_call | solution.py:1059
  103.6 4.2 %finish.1 = f32[2304,1152]{1,0:T(8,128)} custom-call(f32[2304,1152]{1,0:T(8,128)S(1)} %get-tuple-element.8.acc_ref, bf16[8,2304,256]{2,1,0:T(8,128)(2,1)S(1)} %get-tuple-element.9.sa_ref, bf16[4,3,128,256]{3,2,1,0:T(8,128)(2,1)S(1)} %get-tuple-element.10.last_ref), custom_call_target="tpu_custom_call" | custom-call | tf_op jit(solution)/shard_map/finish/pallas_call | solution.py:1143
